TPU v7x, 32 devices: a whole 2x2x4 slice. The times are simulated.
32 devices in a mesh: dp: 2 (over core), seq: 8 (over z, x), mp: 2 (over y).
Axes of the slice: x: 2, y: 2, z: 4, core: 2. Of those that a mesh axis runs over, the one named last changes fastest.
Arguments:
- queries: bfloat16 [4, 1024, 4096], P('dp', 'seq', 'mp'), may hold values from -6 to 6
- vision: bfloat16 [4, 640, 4096], P('dp', 'seq'), may hold values from -6 to 6
- key_weight: bfloat16 [4096, 1024], P(None, 'mp'), may hold values from -0.09375 to 0.09375
- value_weight: bfloat16 [4096, 1024], P(None, 'mp'), may hold values from -0.09375 to 0.09375
- query_gain: float32 [128], replicated, may hold values from 0.6 to 6
- key_gain: float32 [128], replicated, may hold values from 0.6 to 6
- out_grad: bfloat16 [4, 1024, 4096], P('dp', 'seq', 'mp'), may hold values from -6 to 6
- tile_count: int32 [4], P('dp'), may hold values from 1 to 4, as said below
Outputs:
- query_grad: bfloat16 [4, 1024, 4096], P('dp', 'seq', 'mp')
- vision_grad: bfloat16 [4, 640, 4096], P('dp', 'seq', 'mp')
- key_weight_grad: float32 [4096, 1024], P(None, 'mp')
- value_weight_grad: float32 [4096, 1024], P(None, 'mp')
Inputs may be any that keep to these rules, and one draw needn't show every extreme that they name: The live vision tokens of sample s are its first tile_count[s] * 160; some sample has 4 tiles and some other sample has 1.
All inputs are finite; a program needn't handle non-finite values.
Results may differ from a plain program's by a relative error of at most 0.03.
The roundings to bfloat16 on the way count: a program that leaves them out, or rounds other values in their place, can miss the bound.
Values may be sent and summed in bfloat16 or wider, within the bound.
No kernel may reach another device: no remote copies, remote signals or barrier semaphores. Data moves between devices by JAX's collectives and lax.ppermute only.
A program may use at most 128 MiB of HBM per device.

v0:
```python
import functools
import math

import jax
import jax.numpy as jnp
from jax import lax
from jax.experimental import pallas as pl
from jax.experimental.pallas import tpu as pltpu
from jax.sharding import PartitionSpec as P


MAX_TILES = 4
EPS = 1e-05
NEG = -1e30
F32 = jnp.float32
BF16 = jnp.bfloat16


def attention_kernel(blocks, parts, group, head_dim, me_ref, tiles_ref, gain_ref, *refs):
    q_refs, refs = refs[:parts], refs[parts:]
    g_refs, refs = refs[:parts], refs[parts:]
    kv_refs, refs = refs[:blocks], refs[blocks:]
    dq_refs, refs = refs[:parts], refs[parts:]
    dkv_refs, refs = refs[:blocks], refs[blocks:]
    keys, values, dkeys, dvalues = refs
    dq_refs = [dq_refs[0].at[0]] + list(dq_refs[1:])
    rows = kv_refs[0].shape[0]
    total = rows * blocks
    scale = head_dim ** (-0.5)
    token = lax.broadcasted_iota(jnp.int32, (total, 1), 0)
    live = token < 0
    me = me_ref[0]
    live_end = tiles_ref[lax.rem(me, parts)] * (total // MAX_TILES)
    for k in range(blocks):
        keys[k * rows : (k + 1) * rows, :] = kv_refs[k][:, :head_dim]
        values[k * rows : (k + 1) * rows, :] = kv_refs[k][:, head_dim:]
        start = k * rows
        left = live_end - lax.rem(me + blocks - k, blocks) * rows
        live = live | ((token >= start) & (token < start + jnp.minimum(left, rows)))
    bias = jnp.where(live, 0.0, NEG)
    gain = gain_ref[...]
    keys_all = keys[...]
    values_all = values[...]
    keys_turned = keys_all.T
    values_turned = values_all.T
    over_dims = (((1,), (1,)), ((), ()))

    def front(h):
        cols = slice(h * head_dim, (h + 1) * head_dim)
        raw_b = jnp.concatenate([ref[..., cols].reshape(-1, head_dim) for ref in q_refs], axis=0)
        out_b = jnp.concatenate([ref[..., cols].reshape(-1, head_dim) for ref in g_refs], axis=0)
        raw = raw_b.astype(F32)
        inverse = lax.rsqrt(jnp.mean(raw * raw, axis=-1, keepdims=True) + EPS)
        unit = raw * inverse
        normed = (unit * gain).astype(BF16)
        scores = lax.dot_general(keys_all, normed, over_dims, preferred_element_type=F32)
        dprobs = lax.dot_general(values_all, out_b, over_dims, preferred_element_type=F32)
        return cols, out_b, inverse, unit, normed, scores, dprobs

    def middle(cols, out_b, inverse, unit, normed, scores, dprobs):
        scores = scores * (scale * math.log2(math.e)) + bias
        expo = jnp.exp2(scores - jnp.max(scores, axis=0, keepdims=True))
        probs = expo * (1.0 / jnp.sum(expo, axis=0, keepdims=True))
        probs_b = probs.astype(BF16)
        attn = jnp.dot(values_turned, probs_b, preferred_element_type=F32).astype(BF16)
        delta = jnp.sum(out_b.T.astype(F32) * attn.astype(F32), axis=0, keepdims=True)
        dscores = (probs * (dprobs - delta)).astype(BF16)
        return cols, out_b, inverse, unit, normed, probs_b, dscores

    def back(h, cols, out_b, inverse, unit, normed, probs_b, dscores):
        dnormed = jnp.dot(keys_turned, dscores, preferred_element_type=F32).T * scale
        weighted = dnormed * gain
        grad = inverse * (weighted - unit * jnp.mean(weighted * unit, axis=-1, keepdims=True))
        grad = grad.astype(BF16)
        part_rows = grad.shape[0] // parts
        for p in range(parts):
            dq_refs[p][:, cols] = grad[p * part_rows : (p + 1) * part_rows]
        dk = jnp.dot(dscores, normed, preferred_element_type=F32)
        dv = jnp.dot(probs_b, out_b, preferred_element_type=F32)
        if h == 0:
            dkeys[...] = dk
            dvalues[...] = dv
        else:
            dkeys[...] += dk
            dvalues[...] += dv

    ahead = front(0)
    behind = None
    for h in range(group):
        now = ahead
        if h + 1 < group:
            ahead = front(h + 1)
        mid = middle(*now)
        if behind is not None:
            back(h - 1, *behind)
        behind = mid
    back(group - 1, *behind)
    for k in range(blocks):
        span = slice(k * rows, (k + 1) * rows)
        dkv_refs[k][:, :head_dim] = (dkeys[span, :] * scale).astype(BF16)
        dkv_refs[k][:, head_dim:] = dvalues[span, :].astype(BF16)


def attention(me, tiles, gain, queries, out_grad, others, kv_blocks, head_dim):
    blocks = len(kv_blocks)
    parts = 2
    text_rows, width = queries.shape[1:]
    rows, kv_width = kv_blocks[0].shape
    kv_here = kv_width // (2 * head_dim)
    group = width // head_dim // kv_here
    group_width = group * head_dim
    total = rows * blocks
    own = pl.BlockSpec((1, text_rows, group_width), lambda g, m, t: (lax.rem(m[0], parts), 0, g))
    other = pl.BlockSpec((text_rows, group_width), lambda g, m, t: (0, g))
    below = pl.BlockSpec((text_rows, group_width), lambda g, m, t: (1, g))
    kv = pl.BlockSpec((rows, 2 * head_dim), lambda g, m, t: (0, g))
    gain_spec = pl.BlockSpec((1, head_dim), lambda g, m, t: (0, 0))
    work = text_rows * parts * group * kv_here * total
    results = pl.pallas_call(
        functools.partial(attention_kernel, blocks, parts, group, head_dim),
        grid_spec=pltpu.PrefetchScalarGridSpec(
            num_scalar_prefetch=2,
            grid=(kv_here,),
            in_specs=[gain_spec, own, other, own, below] + [kv] * blocks,
            out_specs=[own, other] + [kv] * blocks,
            scratch_shapes=[pltpu.VMEM((total, head_dim), BF16)] * 2
            + [pltpu.VMEM((total, head_dim), F32)] * 2,
        ),
        out_shape=[jax.ShapeDtypeStruct(queries.shape, BF16), jax.ShapeDtypeStruct((text_rows, width), BF16)]
        + [jax.ShapeDtypeStruct((rows, kv_width), BF16)] * blocks,
        cost_estimate=pl.CostEstimate(
            flops=12 * work * head_dim, bytes_accessed=6 * text_rows * parts * width, transcendentals=work
        ),
        name="attention",
    )(me, tiles, gain.reshape(1, head_dim), queries, others, out_grad, others, *kv_blocks)
    return results[:parts], results[parts:]


def project_kernel(samples, head_dim, me_ref, gain_ref, vision_ref, key_ref, value_ref, *refs):
    raw_ref, kv_refs = refs[0], refs[1 : 1 + samples]
    keys, values = refs[1 + samples :]
    step = pl.program_id(0)
    vision = vision_ref[...]
    key_part = jnp.dot(vision, key_ref[...], preferred_element_type=F32)
    value_part = jnp.dot(vision, value_ref[...], preferred_element_type=F32)

    @pl.when(step == 0)
    def _():
        keys[...] = key_part
        values[...] = value_part

    @pl.when(step > 0)
    def _():
        keys[...] += key_part
        values[...] += value_part

    @pl.when(step == pl.num_programs(0) - 1)
    def _():
        raw_ref[...] = keys[...]
        gain = gain_ref[...]
        rows = kv_refs[0].shape[0]
        x = lax.rem(me_ref[0], samples)
        for r in range(samples):
            start = pl.multiple_of(lax.rem(x + r, samples) * rows, 8)
            for h in range(keys.shape[1] // head_dim):
                cols = slice(h * head_dim, (h + 1) * head_dim)
                raw = keys[pl.ds(start, rows), cols]
                inverse = lax.rsqrt(jnp.mean(raw * raw, axis=-1, keepdims=True) + EPS)
                at = 2 * h * head_dim
                kv_refs[r][:, at : at + head_dim] = (raw * inverse * gain).astype(BF16)
                kv_refs[r][:, at + head_dim : at + 2 * head_dim] = values[pl.ds(start, rows), cols].astype(BF16)


def project(me, gain, vision, key_weight, value_weight, samples):
    all_rows, model = vision.shape
    width = key_weight.shape[1]
    head_dim = gain.shape[0]
    rows = all_rows // samples
    step = math.gcd(model, 512)
    weight = pl.BlockSpec((step, width), lambda i, m: (i, 0))
    results = pl.pallas_call(
        functools.partial(project_kernel, samples, head_dim),
        grid_spec=pltpu.PrefetchScalarGridSpec(
            num_scalar_prefetch=1,
            grid=(model // step,),
            in_specs=[
                pl.BlockSpec((1, head_dim), lambda i, m: (0, 0)),
                pl.BlockSpec((all_rows, step), lambda i, m: (0, i)),
                weight,
                weight,
            ],
            out_specs=[pl.BlockSpec((all_rows, width), lambda i, m: (0, 0))]
            + [pl.BlockSpec((rows, 2 * width), lambda i, m: (0, 0))] * samples,
            scratch_shapes=[pltpu.VMEM((all_rows, width), F32)] * 2,
        ),
        out_shape=[jax.ShapeDtypeStruct((all_rows, width), F32)]
        + [jax.ShapeDtypeStruct((rows, 2 * width), BF16)] * samples,
        cost_estimate=pl.CostEstimate(
            flops=4 * all_rows * model * width,
            bytes_accessed=2 * model * (all_rows + 2 * width),
            transcendentals=0,
        ),
        name="project",
    )(me, gain.reshape(1, head_dim), vision, key_weight, value_weight)
    return results[0], results[1:]


def own_grads_kernel(samples, head_dim, me_ref, gain_ref, raw_ref, *refs):
    arrived, out_ref = refs[:-1], refs[-1]
    rows = arrived[0].shape[0]
    width = raw_ref.shape[1]
    gain = gain_ref[...]
    x = lax.rem(me_ref[0], samples)

    def total(r, cols):
        value = arrived[r][:, cols].astype(F32)
        for k in range(r + samples, len(arrived), samples):
            value = value + arrived[k][:, cols].astype(F32)
        return value

    for r in range(samples):
        start = pl.multiple_of(lax.rem(x + r, samples) * rows, 16)
        for h in range(width // head_dim):
            at = h * head_dim
            raw = raw_ref[pl.ds(start, rows), at : at + head_dim]
            inverse = lax.rsqrt(jnp.mean(raw * raw, axis=-1, keepdims=True) + EPS)
            unit = raw * inverse
            weighted = total(r, slice(2 * at, 2 * at + head_dim)) * gain
            grad = inverse * (weighted - unit * jnp.mean(weighted * unit, axis=-1, keepdims=True))
            out_ref[pl.ds(start, rows), at : at + head_dim] = grad.astype(BF16)
            value = total(r, slice(2 * at + head_dim, 2 * (at + head_dim)))
            out_ref[pl.ds(start, rows), width + at : width + at + head_dim] = value.astype(BF16)


def sum_own_grads(me, gain, key_raw, arrived, samples):
    head_dim = gain.shape[0]
    all_rows, width = key_raw.shape
    whole = pl.BlockSpec(memory_space=pltpu.VMEM)
    return pl.pallas_call(
        functools.partial(own_grads_kernel, samples, head_dim),
        in_specs=[pl.BlockSpec(memory_space=pltpu.SMEM)] + [whole] * (2 + len(arrived)),
        out_specs=whole,
        out_shape=jax.ShapeDtypeStruct((all_rows, 2 * width), BF16),
        cost_estimate=pl.CostEstimate(
            flops=40 * all_rows * width * len(arrived), bytes_accessed=4 * all_rows * width * 5, transcendentals=0
        ),
        name="own_grads",
    )(me, gain.reshape(1, head_dim), key_raw, *arrived)


def weight_kernel(n, dps, samples, where_ref, *refs):
    own_vision, direct, crossed = refs[0], refs[1:n], refs[n]
    refs = refs[n + 1 :]
    grads, refs = refs[: n + 1], refs[n + 1 :]
    keep_ref, sent_refs = refs[0], refs[1:dps]
    vision_all, grads_all = refs[dps:]
    mine, helped = where_ref[0], where_ref[1]
    all_rows = own_vision.shape[0]
    rows = all_rows // samples
    vision_all[:all_rows, :] = own_vision[...]
    for k in range(1, n):
        here = pl.multiple_of(k * all_rows + helped * rows, 16)
        there = pl.multiple_of(k * all_rows + (samples - 1 - helped) * rows, 16)
        vision_all[pl.ds(here, rows), :] = direct[k - 1][...]
        vision_all[pl.ds(there, rows), :] = crossed[(k - 1) * rows : k * rows, :]
    at = 0
    for grad in grads:
        grads_all[at : at + grad.shape[0], :] = grad[...]
        at += grad.shape[0]
    piece = keep_ref.shape[0]
    for r in range(dps):
        cols = pl.ds(pl.multiple_of(lax.rem(mine + r, dps) * piece, 128), piece)
        part = lax.dot_general(
            vision_all[:, cols], grads_all[...], (((0,), (0,)), ((), ())), preferred_element_type=F32
        )
        if r == 0:
            keep_ref[...] = part
        else:
            sent_refs[r - 1][...] = part.astype(BF16)


def weight_grads(where, own_vision, direct, crossed, grads, dps, samples):
    n = 1 + len(direct)
    all_rows, share = own_vision.shape
    width = grads[0].shape[1]
    piece = share // dps
    whole = pl.BlockSpec(memory_space=pltpu.VMEM)
    inputs = [own_vision, *direct, crossed, *grads]
    return pl.pallas_call(
        functools.partial(weight_kernel, n, dps, samples),
        in_specs=[pl.BlockSpec(memory_space=pltpu.SMEM)] + [whole] * len(inputs),
        out_specs=[whole] * dps,
        out_shape=[jax.ShapeDtypeStruct((piece, width), F32)]
        + [jax.ShapeDtypeStruct((piece, width), BF16)] * (dps - 1),
        scratch_shapes=[pltpu.VMEM((n * all_rows, share), BF16), pltpu.VMEM((n * all_rows, width), BF16)],
        cost_estimate=pl.CostEstimate(
            flops=2 * n * all_rows * share * width,
            bytes_accessed=2 * n * all_rows * (share + width),
            transcendentals=0,
        ),
        name="weight_grads",
    )(where, *inputs)


def scatter_kernel(pieces, n, share, where_ref, *refs):
    piece_refs, refs = refs[: len(pieces)], refs[len(pieces) :]
    outs, wide, sem = refs[-4:-2], refs[-2], refs[-1]
    half = outs[0].shape[1]
    at, mine = where_ref[0], where_ref[1]
    copies = []
    top = 0
    for p, (steps, side, core, below) in enumerate(pieces):
        rows = piece_refs[p].shape[0]
        place = lax.rem(at + n + steps + side * mine, n)
        core_at = lax.rem(mine + core, 2)
        start = pl.multiple_of(place * share + core_at * (share // 2) + below, 8)
        for q, out in enumerate(outs):
            wide[q, top : top + rows, :] = piece_refs[p][:, q * half : (q + 1) * half].astype(F32)
            copy = pltpu.make_async_copy(
                wide.at[q, pl.ds(top, rows), :], out.at[pl.ds(start, rows), :], sem.at[p, q]
            )
            copy.start()
            copies.append(copy)
        top += rows
    for copy in copies:
        copy.wait()


def scatter_rows(outs, where, values, pieces, n):
    count = len(values)
    rows = sum(v.shape[0] for v in values)
    width = values[0].shape[1] // 2
    whole = pl.BlockSpec(memory_space=pltpu.VMEM)
    share = outs[0].shape[0] // n
    return pl.pallas_call(
        functools.partial(scatter_kernel, pieces, n, share),
        in_specs=[pl.BlockSpec(memory_space=pltpu.SMEM)]
        + [whole] * count
        + [pl.BlockSpec(memory_space=pl.ANY)] * 2,
        out_specs=[pl.BlockSpec(memory_space=pl.ANY)] * 2,
        scratch_shapes=[pltpu.VMEM((2, rows, width), F32), pltpu.SemaphoreType.DMA((count, 2))],
        out_shape=[jax.ShapeDtypeStruct(o.shape, F32) for o in outs],
        input_output_aliases={1 + count: 0, 2 + count: 1},
        cost_estimate=pl.CostEstimate(flops=rows * width * 2000, bytes_accessed=rows * width * 12, transcendentals=0),
        name="scatter_rows",
    )(where, *values, *outs)


def blank_kernel(*refs):
    pass


def blank(shape):
    return pl.pallas_call(
        blank_kernel,
        out_specs=[pl.BlockSpec(memory_space=pl.ANY)] * 2,
        out_shape=[jax.ShapeDtypeStruct(shape, F32)] * 2,
        name="blank",
    )()


def local(sizes, queries, vision, key_weight, value_weight, query_gain, key_gain, out_grad, tile_count):
    n, dps, mps = sizes["seq"], sizes["dp"], sizes["mp"]
    head_dim = query_gain.shape[0]
    samples, rows, model = vision.shape
    width = key_weight.shape[1]
    me, mine, mp = lax.axis_index("seq"), lax.axis_index("dp"), lax.axis_index("mp")
    x = me % samples
    me_ref = me.astype(jnp.int32).reshape(1)
    order = [i for i in range(0, n, 2)] + [i for i in range(n - 1, 0, -2)]
    at = jnp.where(me % 2 == 0, me // 2, n - 1 - me // 2)
    helped = mp % samples

    def shift(value, k):
        return lax.ppermute(value, "seq", [(i, (i + k) % n) for i in range(n)])

    def ring(value, k):
        return lax.ppermute(value, "seq", [(order[i], order[(i + k) % n]) for i in range(n)])

    def within(value, axis, k, size):
        perm = [(i, i // samples * samples + (i % samples + k) % samples) for i in range(size)]
        return lax.ppermute(value, axis, perm)

    def pick(value, i):
        return lax.dynamic_index_in_dim(value, i % samples, 0, False)

    others = within(jnp.concatenate([pick(queries, x + 1), pick(out_grad, x + 1)], axis=0), "seq", 1, n)

    flat_vision = vision.reshape(samples * rows, model)
    key_raw, kv_rel = project(me_ref, key_gain, flat_vision, key_weight, value_weight, samples)
    kv_blocks = [kv_rel[0]]
    for k in range(1, n):
        kv_blocks.append(shift(kv_rel[k % samples], k))

    share = model // n
    sample_vision = pick(vision, helped)
    direct = []
    for k in range(1, n):
        cut = lax.dynamic_slice_in_dim(sample_vision, (at + k) % n * share, share, axis=1)
        direct.append(ring(cut, k))
    own_vision = lax.dynamic_slice_in_dim(flat_vision, at * share, share, axis=1)

    dq, dkv = attention(
        me_ref, tile_count, query_gain, queries, out_grad, others, kv_blocks, head_dim
    )

    arrived = [dkv[0]]
    for k in range(1, n):
        arrived.append(shift(dkv[k], -k))
    returned = within(dq[1], "seq", 1, n)
    direct = lax.optimization_barrier(direct)
    crossed = within(jnp.concatenate(direct, axis=0), "mp", 1, mps)
    own_grads = sum_own_grads(me_ref, key_gain, key_raw, arrived, samples)

    half = own_grads.shape[0] // 2
    grads = [own_grads] + [None] * n
    up = down = own_grads
    for k in range(1, n // 2):
        up, down = ring(up, 1), ring(down, -1)
        grads[k], grads[n + 1 - k] = up, down
    grads[n // 2], grads[n // 2 + 1] = ring(up[:half], 1), ring(down[half:], -1)
    over_cols = (((1,), (1,)), ((), ()))
    full = lax.dot_general(own_grads[:, :width], key_weight, over_cols, preferred_element_type=F32)
    full = full + lax.dot_general(own_grads[:, width:], value_weight, over_cols, preferred_element_type=F32)
    cols = model // mps
    slices = [lax.dynamic_slice_in_dim(full, (mp + k) % mps * cols, cols, axis=1) for k in range(mps)]
    slices = [slices[0]] + [v.astype(BF16) for v in slices[1:]]
    own_vision, slices = lax.optimization_barrier((own_vision, slices))
    vision_grad = slices[0]
    for k in range(1, mps):
        got = lax.ppermute(slices[k], "mp", [(i, (i + k) % mps) for i in range(mps)])
        vision_grad = vision_grad + got.astype(F32)
    vision_grad = vision_grad.astype(BF16).reshape(samples, rows, cols)

    where = jnp.stack([mine, helped]).astype(jnp.int32)
    keep, sent = weight_grads(where, own_vision, direct, crossed, grads, dps, samples)

    def across(value):
        return lax.ppermute(value, "dp", [(i, (i + 1) % dps) for i in range(dps)])

    def split_ring(value):
        perm = []
        for d in range(dps):
            perm += [(d * n + order[i], d * n + order[(i + 1 - 2 * d) % n]) for i in range(n)]
        return lax.ppermute(value, ("dp", "seq"), perm)

    shard = (keep + across(sent).astype(F32)).astype(BF16)
    spot = jnp.stack([at, mine]).astype(jnp.int32)
    query_grad = lax.dynamic_update_index_in_dim(dq[0], returned, (x + 1) % samples, 0)
    values = [shard, across(shard)]
    outs = blank((model, width))
    outs = scatter_rows(outs, spot, values, ((0, 0, 0, 0), (0, 0, 1, 0)), n)
    far = n // 2
    for k in range(1, far + 1):
        for _ in range(dps if k < far else 1):
            values.append(split_ring(values[-dps]))
        new = values[-dps:] if k < far else values[-1:]
        pieces = tuple((-k, 2 * k, core, 0) for core in range(len(new)))
        pieces += tuple((k, -2 * k, 1 - core, 0) for core in range(len(new)))
        crossing = [across(v) for v in new]
        outs = scatter_rows(outs, spot, list(new) + crossing, pieces, n)
    key_weight_grad, value_weight_grad = outs

    query_grad = lax.dynamic_update_index_in_dim(dq[0], returned, (x + 1) % samples, 0)
    return (query_grad, vision_grad, key_weight_grad, value_weight_grad)


def solution(mesh):
    in_specs = (
        P("dp", "seq", "mp"),
        P("dp", "seq", None),
        P(None, "mp"),
        P(None, "mp"),
        P(),
        P(),
        P("dp", "seq", "mp"),
        P("dp"),
    )
    out_specs = (P("dp", "seq", "mp"), P("dp", "seq", "mp"), P(None, "mp"), P(None, "mp"))

    def body(*args):
        return local(dict(mesh.shape), *args)

    return jax.shard_map(body, mesh=mesh, in_specs=in_specs, out_specs=out_specs, check_vma=False)
```

profile of v0, /device:TPU:0, one launch (start us, length us, event | category | flops | bytes accessed | tf_op | source)
XLA Modules:
  0.0 249.2 jit_solution(5475109433218874382)
XLA Ops:
  11.1 3.4 %collective-permute-start.20 = (bf16[80,512]{1,0:T(8,128)(2,1)S(1)}, bf16[80,512]{1,0:T(8,128)(2,1)S(1)}, u32[]{:S(2)}, u32[]{:S(2)}) collective-permute-start(bf16[80,512]{1,0:T(8,128)(2,1)S(1)} %get-tuple-element.80), channel_id=1, source_target_pairs={{0,14},{4,10},{8,6},{12,2},{14,0},{10,4},{6,8},{2,12},{1,15},{5,11... | collective-permute-start | bytes 245768 | tf_op jit(solution)/shard_map/ppermute | solution.py:378
  14.5 20.8 %collective-permute-done.17.refs_1_ = bf16[80,512]{1,0:T(8,128)(2,1)S(1)} collective-permute-done((bf16[80,512]{1,0:T(8,128)(2,1)S(1)}, bf16[80,512]{1,0:T(8,128)(2,1)S(1)}, u32[]{:S(2)}, u32[]{:S(2)}) %collective-permute-start.17) | collective-permute-done | bytes 81952 | tf_op jit(solution)/shard_map/ppermute | solution.py:378
  35.3 8.4 %project.1 = (f32[160,512]{1,0:T(8,128)}, bf16[80,1024]{1,0:T(8,128)(2,1)}, bf16[80,1024]{1,0:T(8,128)(2,1)}) custom-call(s32[1]{0:T(128)} %bitcast.me_ref, f32[1,128]{1,0:T(1,128)} %bitcast.33, bf16[160,4096]{1,0:T(8,128)(2,1)} %bitcast.30, bf16[4096,512]{1,0:T(8,128)(2,1)} %key_ref.1, bf16[4096,512]{1,0:T(8,128)(2,1)} %value_ref.1), custom_call_target="tpu_custom_call" | custom-call | flops 1342177280 | bytes 9699328 | tf_op jit(solution)/shard_map/project/pallas_call | solution.py:181
  43.7 4.3 %collective-permute-start.22 = (bf16[80,512]{1,0:T(8,128)(2,1)S(1)}, bf16[80,512]{1,0:T(8,128)(2,1)S(1)}, u32[]{:S(2)}, u32[]{:S(2)}) collective-permute-start(bf16[80,512]{1,0:T(8,128)(2,1)S(1)} %get-tuple-element.84), channel_id=1, source_target_pairs={{0,6},{4,2},{8,0},{12,4},{14,8},{10,12},{6,14},{2,10},{1,7},{5,3},... | collective-permute-start | bytes 245768 | tf_op jit(solution)/shard_map/ppermute | solution.py:378
  50.6 10.1 %collective-permute-start.23 = (bf16[80,512]{1,0:T(8,128)(2,1)S(1)}, bf16[80,512]{1,0:T(8,128)(2,1)S(1)}, u32[]{:S(2)}, u32[]{:S(2)}) collective-permute-start(bf16[80,512]{1,0:T(8,128)(2,1)S(1)} %get-tuple-element.78), channel_id=1, source_target_pairs={{0,2},{4,0},{8,4},{12,8},{14,12},{10,14},{6,10},{2,6},{1,3},{5,1},... | collective-permute-start | bytes 245768 | tf_op jit(solution)/shard_map/ppermute | solution.py:378
  62.8 7.0 %collective-permute-start.5 = (bf16[80,1024]{1,0:T(8,128)(2,1)}, bf16[80,1024]{1,0:T(8,128)(2,1)S(1)}, u32[]{:S(2)}, u32[]{:S(2)}) collective-permute-start(bf16[80,1024]{1,0:T(8,128)(2,1)} %get-tuple-element.42), channel_id=1, source_target_pairs={{0,10},{2,12},{4,14},{6,0},{8,2},{10,4},{12,6},{14,8},{1,11},{3,13... | collective-permute-start | bytes 491528 | tf_op jit(solution)/shard_map/ppermute | solution.py:375
  75.1 5.3 %collective-permute-done.6.refs_10_ = bf16[80,1024]{1,0:T(8,128)(2,1)S(1)} collective-permute-done((bf16[80,1024]{1,0:T(8,128)(2,1)}, bf16[80,1024]{1,0:T(8,128)(2,1)S(1)}, u32[]{:S(2)}, u32[]{:S(2)}) %collective-permute-start.6) | collective-permute-done | bytes 163872 | tf_op jit(solution)/shard_map/ppermute | solution.py:375
  81.2 13.6 %attention.1 = (bf16[2,128,2048]{2,1,0:T(8,128)(2,1)}, bf16[128,2048]{1,0:T(8,128)(2,1)}, bf16[80,1024]{1,0:T(8,128)(2,1)}, bf16[80,1024]{1,0:T(8,128)(2,1)}, bf...) custom-call(s32[1]{0:T(128)} %bitcast.me_ref, ...), custom_call_target="tpu_custom_call" | custom-call | flops 4026531840 | bytes 3145728 | tf_op jit(solution)/shard_map/attention/pallas_call | solution.py:119
  96.2 5.8 %collective-permute-start.11 = (bf16[80,1024]{1,0:T(8,128)(2,1)}, bf16[80,1024]{1,0:T(8,128)(2,1)S(1)}, u32[]{:S(2)}, u32[]{:S(2)}) collective-permute-start(bf16[80,1024]{1,0:T(8,128)(2,1)} %get-tuple-element.49), channel_id=1, source_target_pairs={{0,10},{2,12},{4,14},{6,0},{8,2},{10,4},{12,6},{14,8},{1,11},{3,13... | collective-permute-start | bytes 491528 | tf_op jit(solution)/shard_map/ppermute | solution.py:375
  108.4 8.9 %collective-permute-start.9 = (bf16[80,1024]{1,0:T(8,128)(2,1)}, bf16[80,1024]{1,0:T(8,128)(2,1)S(1)}, u32[]{:S(2)}, u32[]{:S(2)}) collective-permute-start(bf16[80,1024]{1,0:T(8,128)(2,1)} %get-tuple-element.47), channel_id=1, source_target_pairs={{0,14},{2,0},{4,2},{6,4},{8,6},{10,8},{12,10},{14,12},{1,15},{3,1}... | collective-permute-start | bytes 491528 | tf_op jit(solution)/shard_map/ppermute | solution.py:375
  118.6 6.5 %collective-permute-done.12.refs_4_ = bf16[80,1024]{1,0:T(8,128)(2,1)S(1)} collective-permute-done((bf16[80,1024]{1,0:T(8,128)(2,1)}, bf16[80,1024]{1,0:T(8,128)(2,1)S(1)}, u32[]{:S(2)}, u32[]{:S(2)}) %collective-permute-start.12) | collective-permute-done | bytes 163872 | tf_op jit(solution)/shard_map/ppermute | solution.py:375
  125.1 5.4 %collective-permute-done.13.refs_5_ = bf16[80,1024]{1,0:T(8,128)(2,1)S(1)} collective-permute-done((bf16[80,1024]{1,0:T(8,128)(2,1)}, bf16[80,1024]{1,0:T(8,128)(2,1)S(1)}, u32[]{:S(2)}, u32[]{:S(2)}) %collective-permute-start.13) | collective-permute-done | bytes 163872 | tf_op jit(solution)/shard_map/ppermute | solution.py:375
  144.9 3.9 %fusion = f32[160,4096]{1,0:T(8,128)S(1)} fusion(bf16[4096,512]{1,0:T(8,128)(2,1)} %value_ref.1, bf16[160,1024]{1,0:T(8,128)(2,1)} %own_grads.1.refs_9_), kind=kOutput, calls=%fused_computation.8 | convolution fusion | flops 671088640 | bytes 6979584 | tf_op jit(solution)/shard_map/dot_general | solution.py:424
  167.7 4.6 %weight_grads.1 = (f32[256,1024]{1,0:T(8,128)}, bf16[256,1024]{1,0:T(8,128)(2,1)}) custom-call(s32[2]{0:T(128)} %pad_add_fusion.1.where_ref, bf16[160,512]{1,0:T(8,128)(2,1)} %constant_dynamic-slice_fusion.1.refs_0_, bf16[80,512]{1,0:T(8,128)(2,1)} %copy-done.15, bf16[80,512]{1,0:T(8,128)(2,1)} %copy-done.16, bf16[80,512]{1,0:T(8,128)(2,1)} %copy-done.17, ...), custom_call_target="tpu_custom_call" | custom-call | flops 1342177280 | bytes 3932160 | tf_op jit(solution)/shard_map/weight_grads/pallas_call | solution.py:289
  179.8 5.5 %collective-permute-done.34.refs_0_ = bf16[256,1024]{1,0:T(8,128)(2,1)} collective-permute-done((bf16[256,1024]{1,0:T(8,128)(2,1)S(1)}, bf16[256,1024]{1,0:T(8,128)(2,1)}, u32[]{:S(2)}, u32[]{:S(2)}) %collective-permute-start.34) | collective-permute-done | bytes 524320 | tf_op jit(solution)/shard_map/ppermute | solution.py:445
  187.3 6.5 %collective-permute-done.40.refs_1_ = bf16[256,1024]{1,0:T(8,128)(2,1)} collective-permute-done((bf16[256,1024]{1,0:T(8,128)(2,1)S(1)}, bf16[256,1024]{1,0:T(8,128)(2,1)}, u32[]{:S(2)}, u32[]{:S(2)}) %collective-permute-start.40) | collective-permute-done | bytes 524320 | tf_op jit(solution)/shard_map/ppermute | solution.py:445
  193.8 8.3 %collective-permute-done.35.refs_0_ = bf16[256,1024]{1,0:T(8,128)(2,1)} collective-permute-done((bf16[256,1024]{1,0:T(8,128)(2,1)}, bf16[256,1024]{1,0:T(8,128)(2,1)}, u32[]{:S(2)}, u32[]{:S(2)}) %collective-permute-start.35) | collective-permute-done | bytes 524320 | tf_op jit(solution)/shard_map/ppermute | solution.py:445
  203.7 4.1 %collective-permute-done.8 = bf16[128,2048]{1,0:T(8,128)(2,1)} collective-permute-done((bf16[128,2048]{1,0:T(8,128)(2,1)}, bf16[128,2048]{1,0:T(8,128)(2,1)}, u32[]{:S(2)}, u32[]{:S(2)}) %collective-permute-start.8) | collective-permute-done | bytes 524320 | tf_op jit(solution)/shard_map/ppermute | solution.py:382
  207.8 5.6 %collective-permute-done.41.refs_1_ = bf16[256,1024]{1,0:T(8,128)(2,1)} collective-permute-done((bf16[256,1024]{1,0:T(8,128)(2,1)}, bf16[256,1024]{1,0:T(8,128)(2,1)}, u32[]{:S(2)}, u32[]{:S(2)}) %collective-permute-start.41) | collective-permute-done | bytes 524320 | tf_op jit(solution)/shard_map/ppermute | solution.py:445
  213.4 5.6 %collective-permute-done.36.refs_0_ = bf16[256,1024]{1,0:T(8,128)(2,1)} collective-permute-done((bf16[256,1024]{1,0:T(8,128)(2,1)}, bf16[256,1024]{1,0:T(8,128)(2,1)}, u32[]{:S(2)}, u32[]{:S(2)}) %collective-permute-start.36) | collective-permute-done | bytes 524320 | tf_op jit(solution)/shard_map/ppermute | solution.py:445
  224.6 5.6 %collective-permute-done.37.refs_0_ = bf16[256,1024]{1,0:T(8,128)(2,1)} collective-permute-done((bf16[256,1024]{1,0:T(8,128)(2,1)}, bf16[256,1024]{1,0:T(8,128)(2,1)}, u32[]{:S(2)}, u32[]{:S(2)}) %collective-permute-start.37) | collective-permute-done | bytes 524320 | tf_op jit(solution)/shard_map/ppermute | solution.py:445
  233.8 3.6 %scatter_rows.6 = (f32[4096,512]{1,0:T(8,128)}, f32[4096,512]{1,0:T(8,128)}) custom-call(s32[2]{0:T(128)} %pad_add_fusion.where_ref, bf16[256,1024]{1,0:T(8,128)(2,1)} %collective-permute-done.34.refs_0_, bf16[256,1024]{1,0:T(8,128)(2,1)} %collective-permute-done.40.refs_1_, ...), custom_call_target="tpu_custom_call", output_to_operand_aliasing={{0}: (5, {}), {1}: (6, {})} | custom-call | flops 1048576000 | bytes 6291456 | tf_op jit(solution)/shard_map/scatter_rows/pallas_call | solution.py:335
  237.5 3.7 %scatter_rows.7 = (f32[4096,512]{1,0:T(8,128)}, f32[4096,512]{1,0:T(8,128)}) custom-call(s32[2]{0:T(128)} %pad_add_fusion.where_ref, bf16[256,1024]{1,0:T(8,128)(2,1)} %collective-permute-done.35.refs_0_, bf16[256,1024]{1,0:T(8,128)(2,1)} %collective-permute-done.41.refs_1_, ...), custom_call_target="tpu_custom_call", output_to_operand_aliasing={{0}: (5, {}), {1}: (6, {})} | custom-call | flops 1048576000 | bytes 6291456 | tf_op jit(solution)/shard_map/scatter_rows/pallas_call | solution.py:335
  242.0 3.6 %scatter_rows.8 = (f32[4096,512]{1,0:T(8,128)}, f32[4096,512]{1,0:T(8,128)}) custom-call(s32[2]{0:T(128)} %pad_add_fusion.where_ref, bf16[256,1024]{1,0:T(8,128)(2,1)} %collective-permute-done.36.refs_0_, bf16[256,1024]{1,0:T(8,128)(2,1)} %collective-permute-done.42.refs_1_, ...), custom_call_target="tpu_custom_call", output_to_operand_aliasing={{0}: (5, {}), {1}: (6, {})} | custom-call | flops 1048576000 | bytes 6291456 | tf_op jit(solution)/shard_map/scatter_rows/pallas_call | solution.py:335
  (178 shorter events, 87.8 us)
Async XLA Ops:
  2.0 78.4 %collective-permute-start = (bf16[256,2048]{1,0:T(8,128)(2,1)S(1)}, bf16[256,2048]{1,0:T(8,128)(2,1)}, u32[]{:S(2)}, u32[]{:S(2)}) collective-permute-start(bf16[256,2048]{1,0:T(8,128)(2,1)S(1)} %pad_maximum_fusion), channel_id=1, source_target_pairs={{0,2},{2,0},{4,6},{6,4},{8,10},{10,8},{12,14},{14,12},{1,3},{3,1},... | collective-permute-start | bytes 3145736 | tf_op jit(solution)/shard_map/ppermute | solution.py:382
  6.6 28.7 %collective-permute-start.17 = (bf16[80,512]{1,0:T(8,128)(2,1)S(1)}, bf16[80,512]{1,0:T(8,128)(2,1)S(1)}, u32[]{:S(2)}, u32[]{:S(2)}) collective-permute-start(bf16[80,512]{1,0:T(8,128)(2,1)S(1)} %get-tuple-element.83), channel_id=1, source_target_pairs={{0,4},{4,8},{8,12},{12,14},{14,10},{10,6},{6,2},{2,0},{1,5},{5,9},... | collective-permute-start | bytes 245768 | tf_op jit(solution)/shard_map/ppermute | solution.py:378
  8.2 35.5 %collective-permute-start.18 = (bf16[80,512]{1,0:T(8,128)(2,1)S(1)}, bf16[80,512]{1,0:T(8,128)(2,1)S(1)}, u32[]{:S(2)}, u32[]{:S(2)}) collective-permute-start(bf16[80,512]{1,0:T(8,128)(2,1)S(1)} %get-tuple-element.82), channel_id=1, source_target_pairs={{0,8},{4,12},{8,14},{12,10},{14,6},{10,2},{6,0},{2,4},{1,9},{5,13}... | collective-permute-start | bytes 245768 | tf_op jit(solution)/shard_map/ppermute | solution.py:378
  10.8 37.2 %collective-permute-start.19 = (bf16[80,512]{1,0:T(8,128)(2,1)S(1)}, bf16[80,512]{1,0:T(8,128)(2,1)S(1)}, u32[]{:S(2)}, u32[]{:S(2)}) collective-permute-start(bf16[80,512]{1,0:T(8,128)(2,1)S(1)} %get-tuple-element.81), channel_id=1, source_target_pairs={{0,12},{4,14},{8,10},{12,6},{14,2},{10,0},{6,4},{2,8},{1,13},{5,15... | collective-permute-start | bytes 245768 | tf_op jit(solution)/shard_map/ppermute | solution.py:378
  11.1 38.0 %collective-permute-start.20 = (bf16[80,512]{1,0:T(8,128)(2,1)S(1)}, bf16[80,512]{1,0:T(8,128)(2,1)S(1)}, u32[]{:S(2)}, u32[]{:S(2)}) collective-permute-start(bf16[80,512]{1,0:T(8,128)(2,1)S(1)} %get-tuple-element.80), channel_id=1, source_target_pairs={{0,14},{4,10},{8,6},{12,2},{14,0},{10,4},{6,8},{2,12},{1,15},{5,11... | collective-permute-start | bytes 245768 | tf_op jit(solution)/shard_map/ppermute | solution.py:378
  49.1 20.7 %collective-permute-start.2 = (bf16[80,1024]{1,0:T(8,128)(2,1)}, bf16[80,1024]{1,0:T(8,128)(2,1)S(1)}, u32[]{:S(2)}, u32[]{:S(2)}) collective-permute-start(bf16[80,1024]{1,0:T(8,128)(2,1)} %get-tuple-element.41.refs_4_), channel_id=1, source_target_pairs={{0,4},{2,6},{4,8},{6,10},{8,12},{10,14},{12,0},{14,2},{1,5},{3,7},... | collective-permute-start | bytes 491528 | tf_op jit(solution)/shard_map/ppermute | solution.py:375
  50.6 19.7 %collective-permute-start.3 = (bf16[80,1024]{1,0:T(8,128)(2,1)}, bf16[80,1024]{1,0:T(8,128)(2,1)S(1)}, u32[]{:S(2)}, u32[]{:S(2)}) collective-permute-start(bf16[80,1024]{1,0:T(8,128)(2,1)} %get-tuple-element.42), channel_id=1, source_target_pairs={{0,6},{2,8},{4,10},{6,12},{8,14},{10,0},{12,2},{14,4},{1,7},{3,9},... | collective-permute-start | bytes 491528 | tf_op jit(solution)/shard_map/ppermute | solution.py:375
  103.4 21.7 %collective-permute-start.12 = (bf16[80,1024]{1,0:T(8,128)(2,1)}, bf16[80,1024]{1,0:T(8,128)(2,1)S(1)}, u32[]{:S(2)}, u32[]{:S(2)}) collective-permute-start(bf16[80,1024]{1,0:T(8,128)(2,1)} %get-tuple-element.50), channel_id=1, source_target_pairs={{0,8},{2,10},{4,12},{6,14},{8,0},{10,2},{12,4},{14,6},{1,9},{3,11}... | collective-permute-start | bytes 491528 | tf_op jit(solution)/shard_map/ppermute | solution.py:375
  106.1 24.4 %collective-permute-start.13 = (bf16[80,1024]{1,0:T(8,128)(2,1)}, bf16[80,1024]{1,0:T(8,128)(2,1)S(1)}, u32[]{:S(2)}, u32[]{:S(2)}) collective-permute-start(bf16[80,1024]{1,0:T(8,128)(2,1)} %get-tuple-element.51), channel_id=1, source_target_pairs={{0,6},{2,8},{4,10},{6,12},{8,14},{10,0},{12,2},{14,4},{1,7},{3,9},... | collective-permute-start | bytes 491528 | tf_op jit(solution)/shard_map/ppermute | solution.py:375
  106.1 24.4 %collective-permute-start.14 = (bf16[80,1024]{1,0:T(8,128)(2,1)}, bf16[80,1024]{1,0:T(8,128)(2,1)S(1)}, u32[]{:S(2)}, u32[]{:S(2)}) collective-permute-start(bf16[80,1024]{1,0:T(8,128)(2,1)} %get-tuple-element.52), channel_id=1, source_target_pairs={{0,4},{2,6},{4,8},{6,10},{8,12},{10,14},{12,0},{14,2},{1,5},{3,7},... | collective-permute-start | bytes 491528 | tf_op jit(solution)/shard_map/ppermute | solution.py:375
  106.6 23.8 %collective-permute-start.15 = (bf16[80,1024]{1,0:T(8,128)(2,1)}, bf16[80,1024]{1,0:T(8,128)(2,1)S(1)}, u32[]{:S(2)}, u32[]{:S(2)}) collective-permute-start(bf16[80,1024]{1,0:T(8,128)(2,1)} %get-tuple-element.53), channel_id=1, source_target_pairs={{0,2},{2,4},{4,6},{6,8},{8,10},{10,12},{12,14},{14,0},{1,3},{3,5},... | collective-permute-start | bytes 491528 | tf_op jit(solution)/shard_map/ppermute | solution.py:375
  108.4 22.6 %collective-permute-start.9 = (bf16[80,1024]{1,0:T(8,128)(2,1)}, bf16[80,1024]{1,0:T(8,128)(2,1)S(1)}, u32[]{:S(2)}, u32[]{:S(2)}) collective-permute-start(bf16[80,1024]{1,0:T(8,128)(2,1)} %get-tuple-element.47), channel_id=1, source_target_pairs={{0,14},{2,0},{4,2},{6,4},{8,6},{10,8},{12,10},{14,12},{1,15},{3,1}... | collective-permute-start | bytes 491528 | tf_op jit(solution)/shard_map/ppermute | solution.py:375
  138.2 24.1 %collective-permute-start.24 = (bf16[560,512]{1,0:T(8,128)(2,1)}, bf16[560,512]{1,0:T(8,128)(2,1)S(1)}, u32[]{:S(2)}, u32[]{:S(2)}) collective-permute-start(bf16[560,512]{1,0:T(8,128)(2,1)} %constant_dynamic-update-slice_fusion), channel_id=1, source_target_pairs={{0,1},{1,0},{2,3},{3,2},{4,5},{5,4},{6,7},{7,6},{8,9},{9,8},{10,11... | collective-permute-start | bytes 1720328 | tf_op jit(solution)/shard_map/ppermute | solution.py:382
  178.0 15.8 %collective-permute-start.40 = (bf16[256,1024]{1,0:T(8,128)(2,1)S(1)}, bf16[256,1024]{1,0:T(8,128)(2,1)}, u32[]{:S(2)}, u32[]{:S(2)}) collective-permute-start(bf16[256,1024]{1,0:T(8,128)(2,1)S(1)} %collective-permute-done.39.refs_1_), channel_id=1, source_target_pairs={{0,4},{4,8},{8,12},{12,14},{14,10},{10,6},{6,2},{2,0},{16,18},{20,... | collective-permute-start | bytes 1572872 | tf_op jit(solution)/shard_map/ppermute | solution.py:445
  185.3 16.9 %collective-permute-start.35 = (bf16[256,1024]{1,0:T(8,128)(2,1)}, bf16[256,1024]{1,0:T(8,128)(2,1)}, u32[]{:S(2)}, u32[]{:S(2)}) collective-permute-start(bf16[256,1024]{1,0:T(8,128)(2,1)} %collective-permute-done.34.refs_0_), channel_id=1, source_target_pairs={{0,4},{4,8},{8,12},{12,14},{14,10},{10,6},{6,2},{2,0},{16,18},{20,... | collective-permute-start | bytes 1572872 | tf_op jit(solution)/shard_map/ppermute | solution.py:445
  187.3 20.4 %collective-permute-start.8 = (bf16[128,2048]{1,0:T(8,128)(2,1)}, bf16[128,2048]{1,0:T(8,128)(2,1)}, u32[]{:S(2)}, u32[]{:S(2)}) collective-permute-start(bf16[128,2048]{1,0:T(8,128)(2,1)} %get-tuple-element.44), channel_id=1, source_target_pairs={{0,2},{2,0},{4,6},{6,4},{8,10},{10,8},{12,14},{14,12},{1,3},{3,1},... | collective-permute-start | bytes 1572872 | tf_op jit(solution)/shard_map/ppermute | solution.py:382
  193.8 19.6 %collective-permute-start.41 = (bf16[256,1024]{1,0:T(8,128)(2,1)}, bf16[256,1024]{1,0:T(8,128)(2,1)}, u32[]{:S(2)}, u32[]{:S(2)}) collective-permute-start(bf16[256,1024]{1,0:T(8,128)(2,1)} %collective-permute-done.40.refs_1_), channel_id=1, source_target_pairs={{0,4},{4,8},{8,12},{12,14},{14,10},{10,6},{6,2},{2,0},{16,18},{20,... | collective-permute-start | bytes 1572872 | tf_op jit(solution)/shard_map/ppermute | solution.py:445
  202.1 16.9 %collective-permute-start.36 = (bf16[256,1024]{1,0:T(8,128)(2,1)}, bf16[256,1024]{1,0:T(8,128)(2,1)}, u32[]{:S(2)}, u32[]{:S(2)}) collective-permute-start(bf16[256,1024]{1,0:T(8,128)(2,1)} %collective-permute-done.35.refs_0_), channel_id=1, source_target_pairs={{0,4},{4,8},{8,12},{12,14},{14,10},{10,6},{6,2},{2,0},{16,18},{20,... | collective-permute-start | bytes 1572872 | tf_op jit(solution)/shard_map/ppermute | solution.py:445
  202.1 19.3 %collective-permute-start.16 = (bf16[160,2048]{1,0:T(8,128)(2,1)S(1)}, bf16[160,2048]{1,0:T(8,128)(2,1)S(1)}, u32[]{:S(2)}, u32[]{:S(2)}) collective-permute-start(bf16[160,2048]{1,0:T(8,128)(2,1)S(1)} %dynamic-slice_convert_fusion), channel_id=1, source_target_pairs={{0,1},{1,0},{2,3},{3,2},{4,5},{5,4},{6,7},{7,6},{8,9},{9,8},{10,11... | collective-permute-start | bytes 1966088 | tf_op jit(solution)/shard_map/ppermute | solution.py:431
  203.7 17.8 %collective-permute-start.47 = (bf16[256,1024]{1,0:T(8,128)(2,1)}, bf16[256,1024]{1,0:T(8,128)(2,1)}, u32[]{:S(2)}, u32[]{:S(2)}) collective-permute-start(bf16[256,1024]{1,0:T(8,128)(2,1)} %collective-permute-done.34.refs_0_), channel_id=1, source_target_pairs={{0,16},{16,0},{1,17},{17,1},{2,18},{18,2},{3,19},{19,3},{4,20},{20... | collective-permute-start | bytes 1572872 | tf_op jit(solution)/shard_map/ppermute | solution.py:439
  221.5 16.0 %collective-permute-start.45 = (bf16[256,1024]{1,0:T(8,128)(2,1)}, bf16[256,1024]{1,0:T(8,128)(2,1)}, u32[]{:S(2)}, u32[]{:S(2)}) collective-permute-start(bf16[256,1024]{1,0:T(8,128)(2,1)} %collective-permute-done.35.refs_0_), channel_id=1, source_target_pairs={{0,16},{16,0},{1,17},{17,1},{2,18},{18,2},{3,19},{19,3},{4,20},{20... | collective-permute-start | bytes 1572872 | tf_op jit(solution)/shard_map/ppermute | solution.py:439
  221.5 16.0 %collective-permute-start.46 = (bf16[256,1024]{1,0:T(8,128)(2,1)}, bf16[256,1024]{1,0:T(8,128)(2,1)}, u32[]{:S(2)}, u32[]{:S(2)}) collective-permute-start(bf16[256,1024]{1,0:T(8,128)(2,1)} %collective-permute-done.41.refs_1_), channel_id=1, source_target_pairs={{0,16},{16,0},{1,17},{17,1},{2,18},{18,2},{3,19},{19,3},{4,20},{20... | collective-permute-start | bytes 1572872 | tf_op jit(solution)/shard_map/ppermute | solution.py:439
  222.0 19.2 %collective-permute-start.43 = (bf16[256,1024]{1,0:T(8,128)(2,1)}, bf16[256,1024]{1,0:T(8,128)(2,1)S(1)}, u32[]{:S(2)}, u32[]{:S(2)}) collective-permute-start(bf16[256,1024]{1,0:T(8,128)(2,1)} %collective-permute-done.36.refs_0_), channel_id=1, source_target_pairs={{0,16},{16,0},{1,17},{17,1},{2,18},{18,2},{3,19},{19,3},{4,20},{20... | collective-permute-start | bytes 1572872 | tf_op jit(solution)/shard_map/ppermute | solution.py:439
  224.6 16.6 %collective-permute-start.44 = (bf16[256,1024]{1,0:T(8,128)(2,1)}, bf16[256,1024]{1,0:T(8,128)(2,1)}, u32[]{:S(2)}, u32[]{:S(2)}) collective-permute-start(bf16[256,1024]{1,0:T(8,128)(2,1)} %collective-permute-done.42.refs_1_), channel_id=1, source_target_pairs={{0,16},{16,0},{1,17},{17,1},{2,18},{18,2},{3,19},{19,3},{4,20},{20... | collective-permute-start | bytes 1572872 | tf_op jit(solution)/shard_map/ppermute | solution.py:439
  (61 other events, 1025.1 us)
where the time goes:
time: 250 us; the launch traced here: 249 us
  waiting for transfers between devices  102 us (41%)
  starting transfers between devices  77.5 us (31%)
  Pallas kernels  45.3 us (18%)
  local copies, waits for them, and re-layouts  14.6 us (6%)
  matrix products  5.41 us (2%)
  other arithmetic  3.64 us (1%)
    ppermute x7, waiting for transfers between devices, split_ring(): return lax.ppermute(value, ('dp', 'seq'), perm)  39.7 us
    ppermute x15, waiting for transfers between devices, ring(): lax.ppermute(value, 'seq', [(order[i], order[(i + k) % n]) for i in range...  36.1 us
    ppermute x15, starting transfers between devices, ring(): lax.ppermute(value, 'seq', [(order[i], order[(i + k) % n]) for i in range...  32.7 us
    ppermute x14, starting transfers between devices, shift(): return lax.ppermute(value, 'seq', [(i, (i + k) % n) for i in range(n)])  32.1 us
    ppermute x14, waiting for transfers between devices, shift(): return lax.ppermute(value, 'seq', [(i, (i + k) % n) for i in range(n)])  19.6 us
    pallas_call x5, Pallas kernels, scatter_rows(): pl.pallas_call(functools.partial(scatter_kernel, pieces, n, share), in_sp...  16.1 us
    pallas_call x1, Pallas kernels, attention(): pl.pallas_call(functools.partial(attention_kernel, blocks, parts, group,...  13.6 us
    pallas_call x1, Pallas kernels, project(): pl.pallas_call(functools.partial(project_kernel, samples, head_dim), grid...  8.39 us
  transfers between devices with their start and end apart: 49, of which 25 were waited for; matrix products, arithmetic and copies ran while one was open for 7% of the time, Pallas kernels for 9%

commit v1 on v0

--- a/solution.py
+++ b/solution.py
@@ -19,7 +19,7 @@
 def attention_kernel(blocks, parts, group, head_dim, me_ref, tiles_ref, gain_ref, *refs):
     q_refs, refs = refs[:parts], refs[parts:]
     g_refs, refs = refs[:parts], refs[parts:]
-    kv_refs, refs = refs[:blocks], refs[blocks:]
+    kv_refs, refs = refs[:blocks], refs[-(parts + blocks + 4) :]
     dq_refs, refs = refs[:parts], refs[parts:]
     dkv_refs, refs = refs[:blocks], refs[blocks:]
     keys, values, dkeys, dvalues = refs
@@ -35,7 +35,7 @@
         keys[k * rows : (k + 1) * rows, :] = kv_refs[k][:, :head_dim]
         values[k * rows : (k + 1) * rows, :] = kv_refs[k][:, head_dim:]
         start = k * rows
-        left = live_end - lax.rem(me + blocks - k, blocks) * rows
+        left = live_end - lax.bitwise_xor(me, k) * rows
         live = live | ((token >= start) & (token < start + jnp.minimum(left, rows)))
     bias = jnp.where(live, 0.0, NEG)
     gain = gain_ref[...]
@@ -101,44 +101,49 @@
         dkv_refs[k][:, head_dim:] = dvalues[span, :].astype(BF16)
 
 
-def attention(me, tiles, gain, queries, out_grad, others, kv_blocks, head_dim):
+def attention(me, tiles, gain, queries, out_grad, others, kv_blocks, head_dim, kv_here, first, before):
     blocks = len(kv_blocks)
     parts = 2
     text_rows, width = queries.shape[1:]
     rows, kv_width = kv_blocks[0].shape
-    kv_here = kv_width // (2 * head_dim)
+    heads = kv_width // (2 * head_dim)
     group = width // head_dim // kv_here
     group_width = group * head_dim
     total = rows * blocks
-    own = pl.BlockSpec((1, text_rows, group_width), lambda g, m, t: (lax.rem(m[0], parts), 0, g))
-    other = pl.BlockSpec((text_rows, group_width), lambda g, m, t: (0, g))
-    below = pl.BlockSpec((text_rows, group_width), lambda g, m, t: (1, g))
+    own = pl.BlockSpec((1, text_rows, group_width), lambda g, m, t: (lax.rem(m[0], parts), 0, g + first))
+    other = pl.BlockSpec((text_rows, group_width), lambda g, m, t: (0, g + first))
+    below = pl.BlockSpec((text_rows, group_width), lambda g, m, t: (1, g + first))
     kv = pl.BlockSpec((rows, 2 * head_dim), lambda g, m, t: (0, g))
+    dkv = pl.BlockSpec((rows, 2 * head_dim), lambda g, m, t: (0, g + first))
     gain_spec = pl.BlockSpec((1, head_dim), lambda g, m, t: (0, 0))
-    work = text_rows * parts * group * kv_here * total
+    work = text_rows * parts * group * heads * total
     results = pl.pallas_call(
         functools.partial(attention_kernel, blocks, parts, group, head_dim),
         grid_spec=pltpu.PrefetchScalarGridSpec(
             num_scalar_prefetch=2,
-            grid=(kv_here,),
-            in_specs=[gain_spec, own, other, own, below] + [kv] * blocks,
-            out_specs=[own, other] + [kv] * blocks,
+            grid=(heads,),
+            in_specs=[gain_spec, own, other, own, below]
+            + [kv] * blocks
+            + [pl.BlockSpec(memory_space=pl.ANY)] * len(before),
+            out_specs=[own, other] + [dkv] * blocks,
             scratch_shapes=[pltpu.VMEM((total, head_dim), BF16)] * 2
             + [pltpu.VMEM((total, head_dim), F32)] * 2,
         ),
         out_shape=[jax.ShapeDtypeStruct(queries.shape, BF16), jax.ShapeDtypeStruct((text_rows, width), BF16)]
-        + [jax.ShapeDtypeStruct((rows, kv_width), BF16)] * blocks,
+        + [jax.ShapeDtypeStruct((rows, 2 * head_dim * kv_here), BF16)] * blocks,
+        input_output_aliases={7 + blocks + i: i for i in range(len(before))},
         cost_estimate=pl.CostEstimate(
-            flops=12 * work * head_dim, bytes_accessed=6 * text_rows * parts * width, transcendentals=work
+            flops=12 * work * head_dim,
+            bytes_accessed=6 * text_rows * parts * group_width * heads,
+            transcendentals=work,
         ),
         name="attention",
-    )(me, tiles, gain.reshape(1, head_dim), queries, others, out_grad, others, *kv_blocks)
-    return results[:parts], results[parts:]
-
-
-def project_kernel(samples, head_dim, me_ref, gain_ref, vision_ref, key_ref, value_ref, *refs):
-    raw_ref, kv_refs = refs[0], refs[1 : 1 + samples]
-    keys, values = refs[1 + samples :]
+    )(me, tiles, gain.reshape(1, head_dim), queries, others, out_grad, others, *kv_blocks, *before)
+    return results
+
+
+def project_kernel(samples, chunks, head_dim, me_ref, gain_ref, vision_ref, key_ref, value_ref, *refs):
+    raw_ref, kv_refs, (keys, values) = refs[0], refs[1:-2], refs[-2:]
     step = pl.program_id(0)
     vision = vision_ref[...]
     key_part = jnp.dot(vision, key_ref[...], preferred_element_type=F32)
@@ -162,16 +167,18 @@
         x = lax.rem(me_ref[0], samples)
         for r in range(samples):
             start = pl.multiple_of(lax.rem(x + r, samples) * rows, 8)
-            for h in range(keys.shape[1] // head_dim):
+            heads = keys.shape[1] // head_dim
+            for h in range(heads):
                 cols = slice(h * head_dim, (h + 1) * head_dim)
                 raw = keys[pl.ds(start, rows), cols]
                 inverse = lax.rsqrt(jnp.mean(raw * raw, axis=-1, keepdims=True) + EPS)
-                at = 2 * h * head_dim
-                kv_refs[r][:, at : at + head_dim] = (raw * inverse * gain).astype(BF16)
-                kv_refs[r][:, at + head_dim : at + 2 * head_dim] = values[pl.ds(start, rows), cols].astype(BF16)
-
-
-def project(me, gain, vision, key_weight, value_weight, samples):
+                kv_ref = kv_refs[r * chunks + h * chunks // heads]
+                at = 2 * (h % (heads // chunks)) * head_dim
+                kv_ref[:, at : at + head_dim] = (raw * inverse * gain).astype(BF16)
+                kv_ref[:, at + head_dim : at + 2 * head_dim] = values[pl.ds(start, rows), cols].astype(BF16)
+
+
+def project(me, gain, vision, key_weight, value_weight, samples, chunks):
     all_rows, model = vision.shape
     width = key_weight.shape[1]
     head_dim = gain.shape[0]
@@ -179,7 +186,7 @@
     step = math.gcd(model, 512)
     weight = pl.BlockSpec((step, width), lambda i, m: (i, 0))
     results = pl.pallas_call(
-        functools.partial(project_kernel, samples, head_dim),
+        functools.partial(project_kernel, samples, chunks, head_dim),
         grid_spec=pltpu.PrefetchScalarGridSpec(
             num_scalar_prefetch=1,
             grid=(model // step,),
@@ -190,11 +197,11 @@
                 weight,
             ],
             out_specs=[pl.BlockSpec((all_rows, width), lambda i, m: (0, 0))]
-            + [pl.BlockSpec((rows, 2 * width), lambda i, m: (0, 0))] * samples,
+            + [pl.BlockSpec((rows, 2 * width // chunks), lambda i, m: (0, 0))] * (samples * chunks),
             scratch_shapes=[pltpu.VMEM((all_rows, width), F32)] * 2,
         ),
         out_shape=[jax.ShapeDtypeStruct((all_rows, width), F32)]
-        + [jax.ShapeDtypeStruct((rows, 2 * width), BF16)] * samples,
+        + [jax.ShapeDtypeStruct((rows, 2 * width // chunks), BF16)] * (samples * chunks),
         cost_estimate=pl.CostEstimate(
             flops=4 * all_rows * model * width,
             bytes_accessed=2 * model * (all_rows + 2 * width),
@@ -202,7 +209,7 @@
         ),
         name="project",
     )(me, gain.reshape(1, head_dim), vision, key_weight, value_weight)
-    return results[0], results[1:]
+    return results[0], [results[1 + r * chunks : 1 + (r + 1) * chunks] for r in range(samples)]
 
 
 def own_grads_kernel(samples, head_dim, me_ref, gain_ref, raw_ref, *refs):
@@ -248,25 +255,53 @@
     )(me, gain.reshape(1, head_dim), key_raw, *arrived)
 
 
+def pack_kernel(samples, where_ref, *refs):
+    blocks, (stay_ref, go_ref) = refs[:-2], refs[-2:]
+    x = lax.rem(where_ref[2], samples)
+    rows, share = blocks[0].shape[0], stay_ref.shape[1]
+    for z, block in enumerate(blocks):
+        span = slice(z * rows, (z + 1) * rows)
+        stay_ref[span, :] = block[:, pl.ds(pl.multiple_of(x * share, 128), share)]
+        go_ref[span, :] = block[:, pl.ds(pl.multiple_of((samples - 1 - x) * share, 128), share)]
+
+
+def pack(where, blocks, samples):
+    rows, width = blocks[0].shape
+    whole = pl.BlockSpec(memory_space=pltpu.VMEM)
+    shape = jax.ShapeDtypeStruct((len(blocks) * rows, width // samples), BF16)
+    return pl.pallas_call(
+        functools.partial(pack_kernel, samples),
+        in_specs=[pl.BlockSpec(memory_space=pltpu.SMEM)] + [whole] * len(blocks),
+        out_specs=[whole] * 2,
+        out_shape=[shape] * 2,
+        cost_estimate=pl.CostEstimate(
+            flops=0, bytes_accessed=4 * len(blocks) * rows * width, transcendentals=0
+        ),
+        name="pack",
+    )(where, *blocks)
+
+
 def weight_kernel(n, dps, samples, where_ref, *refs):
-    own_vision, direct, crossed = refs[0], refs[1:n], refs[n]
-    refs = refs[n + 1 :]
-    grads, refs = refs[: n + 1], refs[n + 1 :]
+    vision, grads, refs = refs[:4], refs[4 : n + 4], refs[n + 4 :]
     keep_ref, sent_refs = refs[0], refs[1:dps]
     vision_all, grads_all = refs[dps:]
-    mine, helped = where_ref[0], where_ref[1]
-    all_rows = own_vision.shape[0]
-    rows = all_rows // samples
-    vision_all[:all_rows, :] = own_vision[...]
-    for k in range(1, n):
+    mine, helped, me = where_ref[0], where_ref[1], where_ref[2]
+    rows = vision[0].shape[0] * samples // n
+    all_rows = rows * samples
+
+    def place_of(i):
+        return jnp.where(lax.rem(i, 2) == 0, lax.div(i, 2), n - 1 - lax.div(i, 2))
+
+    for j in range(n):
+        k = lax.rem(place_of(me) + n - place_of(lax.bitwise_xor(me, j)), n)
+        span = slice(j // 2 * rows, (j // 2 + 1) * rows)
         here = pl.multiple_of(k * all_rows + helped * rows, 16)
         there = pl.multiple_of(k * all_rows + (samples - 1 - helped) * rows, 16)
-        vision_all[pl.ds(here, rows), :] = direct[k - 1][...]
-        vision_all[pl.ds(there, rows), :] = crossed[(k - 1) * rows : k * rows, :]
-    at = 0
-    for grad in grads:
-        grads_all[at : at + grad.shape[0], :] = grad[...]
-        at += grad.shape[0]
+        vision_all[pl.ds(here, rows), :] = vision[j % 2][span, :]
+        vision_all[pl.ds(there, rows), :] = vision[2 + j % 2][span, :]
+    for k in range(n):
+        place = jnp.where(mine == 0, k, (n - k) % n)
+        grads_all[pl.ds(pl.multiple_of(place * all_rows, 16), all_rows), :] = grads[k][...]
     piece = keep_ref.shape[0]
     for r in range(dps):
         cols = pl.ds(pl.multiple_of(lax.rem(mine + r, dps) * piece, 128), piece)
@@ -279,13 +314,13 @@
             sent_refs[r - 1][...] = part.astype(BF16)
 
 
-def weight_grads(where, own_vision, direct, crossed, grads, dps, samples):
-    n = 1 + len(direct)
-    all_rows, share = own_vision.shape
+def weight_grads(where, vision, grads, n, dps, samples):
+    share = vision[0].shape[1]
+    all_rows = vision[0].shape[0] * samples * samples // n
     width = grads[0].shape[1]
     piece = share // dps
     whole = pl.BlockSpec(memory_space=pltpu.VMEM)
-    inputs = [own_vision, *direct, crossed, *grads]
+    inputs = [*vision, *grads]
     return pl.pallas_call(
         functools.partial(weight_kernel, n, dps, samples),
         in_specs=[pl.BlockSpec(memory_space=pltpu.SMEM)] + [whole] * len(inputs),
@@ -313,7 +348,8 @@
         rows = piece_refs[p].shape[0]
         place = lax.rem(at + n + steps + side * mine, n)
         core_at = lax.rem(mine + core, 2)
-        start = pl.multiple_of(place * share + core_at * (share // 2) + below, 8)
+        device = jnp.where(place < n // 2, 2 * place, 2 * (n - 1 - place) + 1)
+        start = pl.multiple_of(device * share + core_at * (share // 2) + below, 8)
         for q, out in enumerate(outs):
             wide[q, top : top + rows, :] = piece_refs[p][:, q * half : (q + 1) * half].astype(F32)
             copy = pltpu.make_async_copy(
@@ -368,14 +404,16 @@
     x = me % samples
     me_ref = me.astype(jnp.int32).reshape(1)
     order = [i for i in range(0, n, 2)] + [i for i in range(n - 1, 0, -2)]
-    at = jnp.where(me % 2 == 0, me // 2, n - 1 - me // 2)
     helped = mp % samples
 
-    def shift(value, k):
-        return lax.ppermute(value, "seq", [(i, (i + k) % n) for i in range(n)])
-
-    def ring(value, k):
-        return lax.ppermute(value, "seq", [(order[i], order[(i + k) % n]) for i in range(n)])
+    assert n & (n - 1) == 0 and samples == 2
+    far_first = sorted(range(1, n), key=lambda j: (-((j // 2).bit_length()), -(j // 2), j % 2))
+
+    def swap(value, j):
+        return lax.ppermute(value, "seq", [(i, i ^ j) for i in range(n)])
+
+    def place_of(i):
+        return jnp.where(i % 2 == 0, i // 2, n - 1 - i // 2)
 
     def within(value, axis, k, size):
         perm = [(i, i // samples * samples + (i % samples + k) % samples) for i in range(size)]
@@ -384,65 +422,84 @@
     def pick(value, i):
         return lax.dynamic_index_in_dim(value, i % samples, 0, False)
 
-    others = within(jnp.concatenate([pick(queries, x + 1), pick(out_grad, x + 1)], axis=0), "seq", 1, n)
-
     flat_vision = vision.reshape(samples * rows, model)
-    key_raw, kv_rel = project(me_ref, key_gain, flat_vision, key_weight, value_weight, samples)
-    kv_blocks = [kv_rel[0]]
-    for k in range(1, n):
-        kv_blocks.append(shift(kv_rel[k % samples], k))
+    kv_here = width // head_dim
+    chunks = chunks_of(kv_here)
+    key_raw, kv_rel = project(me_ref, key_gain, flat_vision, key_weight, value_weight, samples, chunks)
+    kv_blocks = []
+    for c in range(chunks):
+        pair = swap(kv_rel[1][c], 1)
+        blocks = [kv_rel[0][c], pair] + [None] * (n - 2)
+        for z in range(n // 2 - 1, 0, -1):
+            blocks[2 * z] = swap(kv_rel[0][c], 2 * z)
+            blocks[2 * z + 1] = swap(pair, 2 * z)
+        kv_blocks.append(blocks)
+
+    others = swap(jnp.concatenate([pick(queries, x + 1), pick(out_grad, x + 1)], axis=0), 1)
 
     share = model // n
+    at = place_of(me)
+    where = jnp.stack([mine, helped, me]).astype(jnp.int32)
     sample_vision = pick(vision, helped)
-    direct = []
-    for k in range(1, n):
-        cut = lax.dynamic_slice_in_dim(sample_vision, (at + k) % n * share, share, axis=1)
-        direct.append(ring(cut, k))
-    own_vision = lax.dynamic_slice_in_dim(flat_vision, at * share, share, axis=1)
-
-    dq, dkv = attention(
-        me_ref, tile_count, query_gain, queries, out_grad, others, kv_blocks, head_dim
-    )
-
-    arrived = [dkv[0]]
-    for k in range(1, n):
-        arrived.append(shift(dkv[k], -k))
+
+    def cut(z):
+        return lax.dynamic_slice_in_dim(sample_vision, z * samples * share, samples * share, axis=1)
+
+    lines = [cut(me // 2)] + [None] * (n // 2 - 1)
+    for z in range(n // 2 - 1, 0, -1):
+        lines[z] = swap(cut(me // 2 ^ z), 2 * z)
+
+    results = []
+    for c in range(chunks):
+        results = attention(
+            me_ref, tile_count, query_gain, queries, out_grad, others, kv_blocks[c], head_dim,
+            kv_here, c * kv_here // chunks, results,
+        )
+    dq, dkv = results[:2], results[2:]
+
+    arrived = [dkv[0]] + [None] * (n - 1)
+    for j in far_first:
+        arrived[j] = swap(dkv[j], j)
     returned = within(dq[1], "seq", 1, n)
-    direct = lax.optimization_barrier(direct)
-    crossed = within(jnp.concatenate(direct, axis=0), "mp", 1, mps)
+    vision_near, going = pack(where, lines, samples)
+    vision_far = swap(going, 1)
+    cross_near = within(vision_near, "mp", 1, mps)
+    cross_far = within(vision_far, "mp", 1, mps)
+    vision_rows = [vision_near, vision_far, cross_near, cross_far]
     own_grads = sum_own_grads(me_ref, key_gain, key_raw, arrived, samples)
 
-    half = own_grads.shape[0] // 2
-    grads = [own_grads] + [None] * n
-    up = down = own_grads
+    def across(value):
+        return lax.ppermute(value, "dp", [(i, (i + 1) % dps) for i in range(dps)])
+
+    def split_ring(value):
+        perm = []
+        for d in range(dps):
+            perm += [(d * n + order[i], d * n + order[(i + 1 - 2 * d) % n]) for i in range(n)]
+        return lax.ppermute(value, ("dp", "seq"), perm)
+
+    grads = [own_grads] + [None] * (n - 1)
+    held = [own_grads, across(own_grads)]
     for k in range(1, n // 2):
-        up, down = ring(up, 1), ring(down, -1)
-        grads[k], grads[n + 1 - k] = up, down
-    grads[n // 2], grads[n // 2 + 1] = ring(up[:half], 1), ring(down[half:], -1)
+        held = [split_ring(v) for v in held]
+        grads[k], grads[n - k] = held[0], across(held[1])
+    grads[n // 2] = split_ring(held[0])
+
     over_cols = (((1,), (1,)), ((), ()))
     full = lax.dot_general(own_grads[:, :width], key_weight, over_cols, preferred_element_type=F32)
     full = full + lax.dot_general(own_grads[:, width:], value_weight, over_cols, preferred_element_type=F32)
     cols = model // mps
     slices = [lax.dynamic_slice_in_dim(full, (mp + k) % mps * cols, cols, axis=1) for k in range(mps)]
     slices = [slices[0]] + [v.astype(BF16) for v in slices[1:]]
-    own_vision, slices = lax.optimization_barrier((own_vision, slices))
+    vision_rows, slices = lax.optimization_barrier((vision_rows, slices))
+    received = []
+    for k in range(1, mps):
+        received.append(lax.ppermute(slices[k], "mp", [(i, (i + k) % mps) for i in range(mps)]))
     vision_grad = slices[0]
-    for k in range(1, mps):
-        got = lax.ppermute(slices[k], "mp", [(i, (i + k) % mps) for i in range(mps)])
+    for got in received:
         vision_grad = vision_grad + got.astype(F32)
     vision_grad = vision_grad.astype(BF16).reshape(samples, rows, cols)
 
-    where = jnp.stack([mine, helped]).astype(jnp.int32)
-    keep, sent = weight_grads(where, own_vision, direct, crossed, grads, dps, samples)
-
-    def across(value):
-        return lax.ppermute(value, "dp", [(i, (i + 1) % dps) for i in range(dps)])
-
-    def split_ring(value):
-        perm = []
-        for d in range(dps):
-            perm += [(d * n + order[i], d * n + order[(i + 1 - 2 * d) % n]) for i in range(n)]
-        return lax.ppermute(value, ("dp", "seq"), perm)
+    keep, sent = weight_grads(where, vision_rows, grads, n, dps, samples)
 
     shard = (keep + across(sent).astype(F32)).astype(BF16)
     spot = jnp.stack([at, mine]).astype(jnp.int32)
@@ -465,6 +522,10 @@
     return (query_grad, vision_grad, key_weight_grad, value_weight_grad)
 
 
+def chunks_of(kv_here):
+    return 2 if kv_here % 2 == 0 else 1
+
+
 def solution(mesh):
     in_specs = (
         P("dp", "seq", "mp"),
@@ -481,4 +542,5 @@
     def body(*args):
         return local(dict(mesh.shape), *args)
 
-    return jax.shard_map(body, mesh=mesh, in_specs=in_specs, out_specs=out_specs, check_vma=False)
+    step = jax.shard_map(body, mesh=mesh, in_specs=in_specs, out_specs=out_specs, check_vma=False)
+    return lambda *args: step(*args)

time: 250 us -> 238 us (0.952)
  starting transfers between devices: 77.5 us -> 69.5 us
  local copies, waits for them, and re-layouts: 14.6 us -> 8.8 us
  Pallas kernels: 45.3 us -> 50 us
  waiting for transfers between devices: 102 us -> 98.7 us
    ppermute x29 -> x26, starting transfers between devices: 64.8 us -> 45.2 us  [swap(): return lax.ppermute(value, 'seq', [(i, i ^ j) for i in range(n)])]
    ppermute x29 -> x26, waiting for transfers between devices: 55.6 us -> 44.3 us  [swap(): return lax.ppermute(value, 'seq', [(i, i ^ j) for i in range(n)])]
    ppermute x7 -> x14, starting transfers between devices: 5.85 us -> 16.1 us  [split_ring(): return lax.ppermute(value, ('dp', 'seq'), perm)]
    ppermute x7 -> x14, waiting for transfers between devices: 39.7 us -> 48.5 us  [split_ring(): return lax.ppermute(value, ('dp', 'seq'), perm)]
    unnamed x78 -> x84, local copies, waits for them, and re-layouts: 7.53 us -> 4.44 us
    pallas_call x1 -> x2, Pallas kernels: 13.6 us -> 16.3 us  [attention(): pl.pallas_call(functools.partial(attention_kernel, blocks, parts, group,...]
    pallas_call x1 -> x2, Pallas kernels: 8.39 us -> 10.4 us  [the longest x1 8.38 us: project(): pl.pallas_call(functools.partial(project_kernel, samples, chunks, head_di...]
  transfers between devices with their start and end apart: 49 -> 57, of which waited for: 25 -> 23; matrix products, arithmetic and copies ran while one was open for 7% -> 4% of each run, Pallas kernels for 9% -> 13%
where the time goes in v1:
time: 238 us; the launch traced here: 237 us
  waiting for transfers between devices  98.7 us (41%)
  starting transfers between devices  69.5 us (29%)
  Pallas kernels  50 us (21%)
  local copies, waits for them, and re-layouts  8.8 us (4%)
  matrix products  5.31 us (2%)
  other arithmetic  3.74 us (2%)
    ppermute x14, waiting for transfers between devices, split_ring(): return lax.ppermute(value, ('dp', 'seq'), perm)  48.5 us
    ppermute x26, starting transfers between devices, swap(): return lax.ppermute(value, 'seq', [(i, i ^ j) for i in range(n)])  45.2 us
    ppermute x26, waiting for transfers between devices, swap(): return lax.ppermute(value, 'seq', [(i, i ^ j) for i in range(n)])  44.3 us
    pallas_call x2, Pallas kernels, attention(): pl.pallas_call(functools.partial(attention_kernel, blocks, parts, group,...  16.3 us
    ppermute x14, starting transfers between devices, split_ring(): return lax.ppermute(value, ('dp', 'seq'), perm)  16.1 us
    pallas_call x5, Pallas kernels, scatter_rows(): pl.pallas_call(functools.partial(scatter_kernel, pieces, n, share), in_sp...  16.1 us
    pallas_call x1, Pallas kernels, project(): pl.pallas_call(functools.partial(project_kernel, samples, chunks, head_di...  8.38 us
  transfers between devices with their start and end apart: 57, of which 23 were waited for; matrix products, arithmetic and copies ran while one was open for 4% of the time, Pallas kernels for 13%

profile of v1, /device:TPU:0, one launch (start us, length us, event | category | flops | bytes accessed | tf_op | source)
XLA Modules:
  0.0 237.4 jit_solution(11279860441742951080)
XLA Ops:
  5.1 8.4 %project.1 = (f32[160,512]{1,0:T(8,128)}, bf16[80,512]{1,0:T(8,128)(2,1)}, bf16[80,512]{1,0:T(8,128)(2,1)}, bf16[80,512]{1,0:T(8,128)(2,1)}, bf16[80,512]{1,0:T(8,128)(2,1)}) custom-call(s32[1]{0:T(128)} %bitcast.me_ref, f32[1,128]{1,0:T(1,128)} %bitcast.26, bf16[160,4096]{1,0:T(8,128)(2,1)} %bitcast.24, bf16[4096,512]{1,0:T(8,128)(2,1)} %key_ref.1, ...), custom_call_target="tpu_custom_call" | custom-call | flops 1342177280 | bytes 9699328 | tf_op jit(solution)/shard_map/project/pallas_call | solution.py:188
  18.2 11.8 %collective-permute-done.8.refs_5_ = bf16[80,512]{1,0:T(8,128)(2,1)S(1)} collective-permute-done((bf16[80,512]{1,0:T(8,128)(2,1)}, bf16[80,512]{1,0:T(8,128)(2,1)S(1)}, u32[]{:S(2)}, u32[]{:S(2)}) %collective-permute-start.8) | collective-permute-done | bytes 81952 | tf_op jit(solution)/shard_map/ppermute | solution.py:413
  45.3 5.7 %collective-permute-start.5 = (bf16[80,512]{1,0:T(8,128)(2,1)S(1)}, bf16[80,512]{1,0:T(8,128)(2,1)S(1)}, u32[]{:S(2)}, u32[]{:S(2)}) collective-permute-start(bf16[80,512]{1,0:T(8,128)(2,1)S(1)} %collective-permute-done.1.refs_5_), channel_id=1, source_target_pairs={{0,8},{2,10},{4,12},{6,14},{8,0},{10,2},{12,4},{14,6},{1,9},{3,11}... | collective-permute-start | bytes 245768 | tf_op jit(solution)/shard_map/ppermute | solution.py:413
  52.0 8.1 %attention.2 = (bf16[2,128,2048]{2,1,0:T(8,128)(2,1)}, bf16[128,2048]{1,0:T(8,128)(2,1)}, bf16[80,1024]{1,0:T(8,128)(2,1)}, bf16[80,1024]{1,0:T(8,128)(2,1)}, bf...) custom-call(s32[1]{0:T(128)} %bitcast.me_ref, ...), custom_call_target="tpu_custom_call" | custom-call | flops 2013265920 | bytes 1572864 | tf_op jit(solution)/shard_map/attention/pallas_call | solution.py:120
  60.9 8.2 %attention.3 = (bf16[2,128,2048]{2,1,0:T(8,128)(2,1)}, bf16[128,2048]{1,0:T(8,128)(2,1)}, bf16[80,1024]{1,0:T(8,128)(2,1)}, bf16[80,1024]{1,0:T(8,128)(2,1)}, bf...) custom-call(s32[1]{0:T(128)} %bitcast.me_ref, ...), custom_call_target="tpu_custom_call", output_to_operand_aliasing={{0}: (15, {}), {1}: (16, {}), {2}: (17, {}), {3}: (18, {}),... | custom-call | flops 2013265920 | bytes 1572864 | tf_op jit(solution)/shard_map/attention/pallas_call | solution.py:120
  79.8 3.2 %collective-permute-done.23.refs_2_ = bf16[80,1024]{1,0:T(8,128)(2,1)S(1)} collective-permute-done((bf16[80,1024]{1,0:T(8,128)(2,1)}, bf16[80,1024]{1,0:T(8,128)(2,1)S(1)}, u32[]{:S(2)}, u32[]{:S(2)}) %collective-permute-start.23) | collective-permute-done | bytes 163872 | tf_op jit(solution)/shard_map/ppermute | solution.py:413
  83.0 7.7 %collective-permute-done.25.refs_4_ = bf16[80,1024]{1,0:T(8,128)(2,1)S(1)} collective-permute-done((bf16[80,1024]{1,0:T(8,128)(2,1)}, bf16[80,1024]{1,0:T(8,128)(2,1)S(1)}, u32[]{:S(2)}, u32[]{:S(2)}) %collective-permute-start.25) | collective-permute-done | bytes 163872 | tf_op jit(solution)/shard_map/ppermute | solution.py:413
  90.7 5.4 %collective-permute-done.26.refs_5_ = bf16[80,1024]{1,0:T(8,128)(2,1)S(1)} collective-permute-done((bf16[80,1024]{1,0:T(8,128)(2,1)}, bf16[80,1024]{1,0:T(8,128)(2,1)S(1)}, u32[]{:S(2)}, u32[]{:S(2)}) %collective-permute-start.26) | collective-permute-done | bytes 163872 | tf_op jit(solution)/shard_map/ppermute | solution.py:413
  100.4 4.1 %collective-permute-start.16 = (bf16[80,1024]{1,0:T(8,128)(2,1)S(1)}, bf16[80,1024]{1,0:T(8,128)(2,1)S(1)}, u32[]{:S(2)}, u32[]{:S(2)}) collective-permute-start(bf16[80,1024]{1,0:T(8,128)(2,1)S(1)} %get-tuple-element.99), channel_id=1, source_target_pairs={{0,4},{2,6},{4,0},{6,2},{8,12},{10,14},{12,8},{14,10},{1,5},{3,7},... | collective-permute-start | bytes 491528 | tf_op jit(solution)/shard_map/ppermute | solution.py:413
  107.5 3.7 %collective-permute-done.16.refs_1_ = bf16[80,1024]{1,0:T(8,128)(2,1)S(1)} collective-permute-done((bf16[80,1024]{1,0:T(8,128)(2,1)S(1)}, bf16[80,1024]{1,0:T(8,128)(2,1)S(1)}, u32[]{:S(2)}, u32[]{:S(2)}) %collective-permute-start.16) | collective-permute-done | bytes 163872 | tf_op jit(solution)/shard_map/ppermute | solution.py:413
  111.2 8.3 %collective-permute-done.17.refs_2_ = bf16[80,1024]{1,0:T(8,128)(2,1)S(1)} collective-permute-done((bf16[80,1024]{1,0:T(8,128)(2,1)S(1)}, bf16[80,1024]{1,0:T(8,128)(2,1)S(1)}, u32[]{:S(2)}, u32[]{:S(2)}) %collective-permute-start.17) | collective-permute-done | bytes 163872 | tf_op jit(solution)/shard_map/ppermute | solution.py:413
  122.7 3.2 %collective-permute-start.30 = (bf16[160,1024]{1,0:T(8,128)(2,1)}, bf16[160,1024]{1,0:T(8,128)(2,1)S(1)}, u32[]{:S(2)}, u32[]{:S(2)}) collective-permute-start(bf16[160,1024]{1,0:T(8,128)(2,1)} %own_grads.1.refs_4_), channel_id=1, source_target_pairs={{0,4},{4,8},{8,12},{12,14},{14,10},{10,6},{6,2},{2,0},{16,18},{20,... | collective-permute-start | bytes 983048 | tf_op jit(solution)/shard_map/ppermute | solution.py:478
  137.7 3.8 %fusion = f32[160,4096]{1,0:T(8,128)S(1)} fusion(bf16[4096,512]{1,0:T(8,128)(2,1)} %value_ref.1, bf16[160,1024]{1,0:T(8,128)(2,1)} %own_grads.1.refs_4_), kind=kOutput, calls=%fused_computation.8 | convolution fusion | flops 671088640 | bytes 6979584 | tf_op jit(solution)/shard_map/dot_general | solution.py:489
  157.5 4.6 %weight_grads.1 = (f32[256,1024]{1,0:T(8,128)}, bf16[256,1024]{1,0:T(8,128)(2,1)}) custom-call(s32[3]{0:T(128)} %pad_add_fusion.where_ref, bf16[320,512]{1,0:T(8,128)(2,1)} %get-tuple-element.80.refs_0_, bf16[320,512]{1,0:T(8,128)(2,1)} %copy-done.26, bf16[320,512]{1,0:T(8,128)(2,1)} %copy-done.28, bf16[320,512]{1,0:T(8,128)(2,1)} %copy-done.29, ...), custom_call_target="tpu_custom_call" | custom-call | flops 1342177280 | bytes 3932160 | tf_op jit(solution)/shard_map/weight_grads/pallas_call | solution.py:324
  169.0 6.0 %collective-permute-done.42.refs_0_ = bf16[256,1024]{1,0:T(8,128)(2,1)S(1)} collective-permute-done((bf16[256,1024]{1,0:T(8,128)(2,1)S(1)}, bf16[256,1024]{1,0:T(8,128)(2,1)S(1)}, u32[]{:S(2)}, u32[]{:S(2)}) %collective-permute-start.42) | collective-permute-done | bytes 524320 | tf_op jit(solution)/shard_map/ppermute | solution.py:478
  177.1 5.5 %collective-permute-done.48.refs_1_ = bf16[256,1024]{1,0:T(8,128)(2,1)} collective-permute-done((bf16[256,1024]{1,0:T(8,128)(2,1)S(1)}, bf16[256,1024]{1,0:T(8,128)(2,1)}, u32[]{:S(2)}, u32[]{:S(2)}) %collective-permute-start.48) | collective-permute-done | bytes 524320 | tf_op jit(solution)/shard_map/ppermute | solution.py:478
  182.6 9.4 %collective-permute-done.43.refs_0_ = bf16[256,1024]{1,0:T(8,128)(2,1)} collective-permute-done((bf16[256,1024]{1,0:T(8,128)(2,1)S(1)}, bf16[256,1024]{1,0:T(8,128)(2,1)}, u32[]{:S(2)}, u32[]{:S(2)}) %collective-permute-start.43) | collective-permute-done | bytes 524320 | tf_op jit(solution)/shard_map/ppermute | solution.py:478
  194.2 3.4 %collective-permute-done.15 = bf16[128,2048]{1,0:T(8,128)(2,1)} collective-permute-done((bf16[128,2048]{1,0:T(8,128)(2,1)}, bf16[128,2048]{1,0:T(8,128)(2,1)}, u32[]{:S(2)}, u32[]{:S(2)}) %collective-permute-start.15) | collective-permute-done | bytes 524320 | tf_op jit(solution)/shard_map/ppermute | solution.py:420
  197.6 5.6 %collective-permute-done.49.refs_1_ = bf16[256,1024]{1,0:T(8,128)(2,1)} collective-permute-done((bf16[256,1024]{1,0:T(8,128)(2,1)}, bf16[256,1024]{1,0:T(8,128)(2,1)}, u32[]{:S(2)}, u32[]{:S(2)}) %collective-permute-start.49) | collective-permute-done | bytes 524320 | tf_op jit(solution)/shard_map/ppermute | solution.py:478
  203.2 5.6 %collective-permute-done.44.refs_0_ = bf16[256,1024]{1,0:T(8,128)(2,1)} collective-permute-done((bf16[256,1024]{1,0:T(8,128)(2,1)}, bf16[256,1024]{1,0:T(8,128)(2,1)}, u32[]{:S(2)}, u32[]{:S(2)}) %collective-permute-start.44) | collective-permute-done | bytes 524320 | tf_op jit(solution)/shard_map/ppermute | solution.py:478
  214.5 5.6 %collective-permute-done.45.refs_0_ = bf16[256,1024]{1,0:T(8,128)(2,1)} collective-permute-done((bf16[256,1024]{1,0:T(8,128)(2,1)}, bf16[256,1024]{1,0:T(8,128)(2,1)}, u32[]{:S(2)}, u32[]{:S(2)}) %collective-permute-start.45) | collective-permute-done | bytes 524320 | tf_op jit(solution)/shard_map/ppermute | solution.py:478
  223.7 3.6 %scatter_rows.6 = (f32[4096,512]{1,0:T(8,128)}, f32[4096,512]{1,0:T(8,128)}) custom-call(s32[2]{0:T(128)} %pad_add_fusion.1.where_ref, bf16[256,1024]{1,0:T(8,128)(2,1)} %copy-done.7, bf16[256,1024]{1,0:T(8,128)(2,1)} %collective-permute-done.48.refs_1_, ...), custom_call_target="tpu_custom_call", output_to_operand_aliasing={{0}: (5, {}), {1}: (6, {})} | custom-call | flops 1048576000 | bytes 6291456 | tf_op jit(solution)/shard_map/scatter_rows/pallas_call | solution.py:371
  227.3 3.6 %scatter_rows.7 = (f32[4096,512]{1,0:T(8,128)}, f32[4096,512]{1,0:T(8,128)}) custom-call(s32[2]{0:T(128)} %pad_add_fusion.1.where_ref, bf16[256,1024]{1,0:T(8,128)(2,1)} %collective-permute-done.43.refs_0_, bf16[256,1024]{1,0:T(8,128)(2,1)} %collective-permute-done.49.refs_1_, ...), custom_call_target="tpu_custom_call", output_to_operand_aliasing={{0}: (5, {}), {1}: (6, {})} | custom-call | flops 1048576000 | bytes 6291456 | tf_op jit(solution)/shard_map/scatter_rows/pallas_call | solution.py:371
  231.0 3.6 %scatter_rows.8 = (f32[4096,512]{1,0:T(8,128)}, f32[4096,512]{1,0:T(8,128)}) custom-call(s32[2]{0:T(128)} %pad_add_fusion.1.where_ref, bf16[256,1024]{1,0:T(8,128)(2,1)} %collective-permute-done.44.refs_0_, bf16[256,1024]{1,0:T(8,128)(2,1)} %collective-permute-done.50.refs_1_, ...), custom_call_target="tpu_custom_call", output_to_operand_aliasing={{0}: (5, {}), {1}: (6, {})} | custom-call | flops 1048576000 | bytes 6291456 | tf_op jit(solution)/shard_map/scatter_rows/pallas_call | solution.py:371
  (198 shorter events, 97.8 us)
Async XLA Ops:
  2.0 49.0 %collective-permute-start = (bf16[256,2048]{1,0:T(8,128)(2,1)S(1)}, bf16[256,2048]{1,0:T(8,128)(2,1)S(1)}, u32[]{:S(2)}, u32[]{:S(2)}) collective-permute-start(bf16[256,2048]{1,0:T(8,128)(2,1)S(1)} %pad_maximum_fusion), channel_id=1, source_target_pairs={{0,2},{2,0},{4,6},{6,4},{8,10},{10,8},{12,14},{14,12},{1,3},{3,1},... | collective-permute-start | bytes 3145736 | tf_op jit(solution)/shard_map/ppermute | solution.py:413
  13.5 16.5 %collective-permute-start.8 = (bf16[80,512]{1,0:T(8,128)(2,1)}, bf16[80,512]{1,0:T(8,128)(2,1)S(1)}, u32[]{:S(2)}, u32[]{:S(2)}) collective-permute-start(bf16[80,512]{1,0:T(8,128)(2,1)} %get-tuple-element.54), channel_id=1, source_target_pairs={{0,2},{2,0},{4,6},{6,4},{8,10},{10,8},{12,14},{14,12},{1,3},{3,1},... | collective-permute-start | bytes 245768 | tf_op jit(solution)/shard_map/ppermute | solution.py:413
  13.5 18.2 %collective-permute-start.11 = (bf16[80,512]{1,0:T(8,128)(2,1)}, bf16[80,512]{1,0:T(8,128)(2,1)S(1)}, u32[]{:S(2)}, u32[]{:S(2)}) collective-permute-start(bf16[80,512]{1,0:T(8,128)(2,1)} %get-tuple-element.53.refs_4_), channel_id=1, source_target_pairs={{0,8},{2,10},{4,12},{6,14},{8,0},{10,2},{12,4},{14,6},{1,9},{3,11}... | collective-permute-start | bytes 245768 | tf_op jit(solution)/shard_map/ppermute | solution.py:413
  16.6 16.7 %collective-permute-start.13 = (bf16[80,512]{1,0:T(8,128)(2,1)}, bf16[80,512]{1,0:T(8,128)(2,1)S(1)}, u32[]{:S(2)}, u32[]{:S(2)}) collective-permute-start(bf16[80,512]{1,0:T(8,128)(2,1)} %get-tuple-element.53.refs_4_), channel_id=1, source_target_pairs={{0,12},{2,14},{4,8},{6,10},{8,4},{10,6},{12,0},{14,2},{1,13},{3,15... | collective-permute-start | bytes 245768 | tf_op jit(solution)/shard_map/ppermute | solution.py:413
  17.9 15.8 %collective-permute-start.9 = (bf16[80,512]{1,0:T(8,128)(2,1)}, bf16[80,512]{1,0:T(8,128)(2,1)S(1)}, u32[]{:S(2)}, u32[]{:S(2)}) collective-permute-start(bf16[80,512]{1,0:T(8,128)(2,1)} %get-tuple-element.53.refs_4_), channel_id=1, source_target_pairs={{0,4},{2,6},{4,0},{6,2},{8,12},{10,14},{12,8},{14,10},{1,5},{3,7},... | collective-permute-start | bytes 245768 | tf_op jit(solution)/shard_map/ppermute | solution.py:413
  38.5 21.6 %collective-permute-start.4 = (bf16[80,512]{1,0:T(8,128)(2,1)}, bf16[80,512]{1,0:T(8,128)(2,1)S(1)}, u32[]{:S(2)}, u32[]{:S(2)}) collective-permute-start(bf16[80,512]{1,0:T(8,128)(2,1)} %get-tuple-element.51.refs_4_), channel_id=1, source_target_pairs={{0,8},{2,10},{4,12},{6,14},{8,0},{10,2},{12,4},{14,6},{1,9},{3,11}... | collective-permute-start | bytes 245768 | tf_op jit(solution)/shard_map/ppermute | solution.py:413
  39.9 20.3 %collective-permute-start.6 = (bf16[80,512]{1,0:T(8,128)(2,1)}, bf16[80,512]{1,0:T(8,128)(2,1)S(1)}, u32[]{:S(2)}, u32[]{:S(2)}) collective-permute-start(bf16[80,512]{1,0:T(8,128)(2,1)} %get-tuple-element.51.refs_4_), channel_id=1, source_target_pairs={{0,12},{2,14},{4,8},{6,10},{8,4},{10,6},{12,0},{14,2},{1,13},{3,15... | collective-permute-start | bytes 245768 | tf_op jit(solution)/shard_map/ppermute | solution.py:413
  44.6 15.5 %collective-permute-start.3 = (bf16[80,512]{1,0:T(8,128)(2,1)S(1)}, bf16[80,512]{1,0:T(8,128)(2,1)S(1)}, u32[]{:S(2)}, u32[]{:S(2)}) collective-permute-start(bf16[80,512]{1,0:T(8,128)(2,1)S(1)} %collective-permute-done.1.refs_5_), channel_id=1, source_target_pairs={{0,4},{2,6},{4,0},{6,2},{8,12},{10,14},{12,8},{14,10},{1,5},{3,7},... | collective-permute-start | bytes 245768 | tf_op jit(solution)/shard_map/ppermute | solution.py:413
  72.7 18.0 %collective-permute-start.25 = (bf16[80,1024]{1,0:T(8,128)(2,1)}, bf16[80,1024]{1,0:T(8,128)(2,1)S(1)}, u32[]{:S(2)}, u32[]{:S(2)}) collective-permute-start(bf16[80,1024]{1,0:T(8,128)(2,1)} %get-tuple-element.74), channel_id=1, source_target_pairs={{0,8},{2,10},{4,12},{6,14},{8,0},{10,2},{12,4},{14,6},{1,9},{3,11}... | collective-permute-start | bytes 491528 | tf_op jit(solution)/shard_map/ppermute | solution.py:413
  74.5 21.6 %collective-permute-start.26 = (bf16[80,1024]{1,0:T(8,128)(2,1)}, bf16[80,1024]{1,0:T(8,128)(2,1)S(1)}, u32[]{:S(2)}, u32[]{:S(2)}) collective-permute-start(bf16[80,1024]{1,0:T(8,128)(2,1)} %get-tuple-element.75), channel_id=1, source_target_pairs={{0,10},{2,8},{4,14},{6,12},{8,2},{10,0},{12,6},{14,4},{1,11},{3,9}... | collective-permute-start | bytes 491528 | tf_op jit(solution)/shard_map/ppermute | solution.py:413
  76.8 19.3 %collective-permute-start.27 = (bf16[80,1024]{1,0:T(8,128)(2,1)}, bf16[80,1024]{1,0:T(8,128)(2,1)S(1)}, u32[]{:S(2)}, u32[]{:S(2)}) collective-permute-start(bf16[80,1024]{1,0:T(8,128)(2,1)} %get-tuple-element.76), channel_id=1, source_target_pairs={{0,12},{2,14},{4,8},{6,10},{8,4},{10,6},{12,0},{14,2},{1,13},{3,15... | collective-permute-start | bytes 491528 | tf_op jit(solution)/shard_map/ppermute | solution.py:413
  99.4 26.5 %collective-permute-start.34 = (bf16[160,1024]{1,0:T(8,128)(2,1)}, bf16[160,1024]{1,0:T(8,128)(2,1)S(1)}, u32[]{:S(2)}, u32[]{:S(2)}) collective-permute-start(bf16[160,1024]{1,0:T(8,128)(2,1)} %own_grads.1.refs_4_), channel_id=1, source_target_pairs={{0,16},{16,0},{1,17},{17,1},{2,18},{18,2},{3,19},{19,3},{4,20},{20... | collective-permute-start | bytes 983048 | tf_op jit(solution)/shard_map/ppermute | solution.py:472
  127.3 21.2 %collective-permute-start.20 = (bf16[320,512]{1,0:T(8,128)(2,1)}, bf16[320,512]{1,0:T(8,128)(2,1)S(1)}, u32[]{:S(2)}, u32[]{:S(2)}) collective-permute-start(bf16[320,512]{1,0:T(8,128)(2,1)} %get-tuple-element.80.refs_0_), channel_id=1, source_target_pairs={{0,1},{1,0},{2,3},{3,2},{4,5},{5,4},{6,7},{7,6},{8,9},{9,8},{10,11... | collective-permute-start | bytes 983048 | tf_op jit(solution)/shard_map/ppermute | solution.py:420
  131.1 22.1 %collective-permute-start.21 = (bf16[320,512]{1,0:T(8,128)(2,1)S(1)}, bf16[320,512]{1,0:T(8,128)(2,1)S(1)}, u32[]{:S(2)}, u32[]{:S(2)}) collective-permute-start(bf16[320,512]{1,0:T(8,128)(2,1)S(1)} %collective-permute-done.19.refs_1_), channel_id=1, source_target_pairs={{0,1},{1,0},{2,3},{3,2},{4,5},{5,4},{6,7},{7,6},{8,9},{9,8},{10,11... | collective-permute-start | bytes 983048 | tf_op jit(solution)/shard_map/ppermute | solution.py:420
  175.0 17.0 %collective-permute-start.43 = (bf16[256,1024]{1,0:T(8,128)(2,1)S(1)}, bf16[256,1024]{1,0:T(8,128)(2,1)}, u32[]{:S(2)}, u32[]{:S(2)}) collective-permute-start(bf16[256,1024]{1,0:T(8,128)(2,1)S(1)} %collective-permute-done.42.refs_0_), channel_id=1, source_target_pairs={{0,4},{4,8},{8,12},{12,14},{14,10},{10,6},{6,2},{2,0},{16,18},{20,... | collective-permute-start | bytes 1572872 | tf_op jit(solution)/shard_map/ppermute | solution.py:478
  176.5 21.1 %collective-permute-start.15 = (bf16[128,2048]{1,0:T(8,128)(2,1)}, bf16[128,2048]{1,0:T(8,128)(2,1)}, u32[]{:S(2)}, u32[]{:S(2)}) collective-permute-start(bf16[128,2048]{1,0:T(8,128)(2,1)} %get-tuple-element.66), channel_id=1, source_target_pairs={{0,2},{2,0},{4,6},{6,4},{8,10},{10,8},{12,14},{14,12},{1,3},{3,1},... | collective-permute-start | bytes 1572872 | tf_op jit(solution)/shard_map/ppermute | solution.py:420
  182.6 20.6 %collective-permute-start.49 = (bf16[256,1024]{1,0:T(8,128)(2,1)}, bf16[256,1024]{1,0:T(8,128)(2,1)}, u32[]{:S(2)}, u32[]{:S(2)}) collective-permute-start(bf16[256,1024]{1,0:T(8,128)(2,1)} %collective-permute-done.48.refs_1_), channel_id=1, source_target_pairs={{0,4},{4,8},{8,12},{12,14},{14,10},{10,6},{6,2},{2,0},{16,18},{20,... | collective-permute-start | bytes 1572872 | tf_op jit(solution)/shard_map/ppermute | solution.py:478
  192.0 16.9 %collective-permute-start.44 = (bf16[256,1024]{1,0:T(8,128)(2,1)}, bf16[256,1024]{1,0:T(8,128)(2,1)}, u32[]{:S(2)}, u32[]{:S(2)}) collective-permute-start(bf16[256,1024]{1,0:T(8,128)(2,1)} %collective-permute-done.43.refs_0_), channel_id=1, source_target_pairs={{0,4},{4,8},{8,12},{12,14},{14,10},{10,6},{6,2},{2,0},{16,18},{20,... | collective-permute-start | bytes 1572872 | tf_op jit(solution)/shard_map/ppermute | solution.py:478
  192.0 18.6 %collective-permute-start.29 = (bf16[160,2048]{1,0:T(8,128)(2,1)}, bf16[160,2048]{1,0:T(8,128)(2,1)S(1)}, u32[]{:S(2)}, u32[]{:S(2)}) collective-permute-start(bf16[160,2048]{1,0:T(8,128)(2,1)} %dynamic-slice_convert_fusion), channel_id=1, source_target_pairs={{0,1},{1,0},{2,3},{3,2},{4,5},{5,4},{6,7},{7,6},{8,9},{9,8},{10,11... | collective-permute-start | bytes 1966088 | tf_op jit(solution)/shard_map/ppermute | solution.py:496
  193.3 18.3 %collective-permute-start.55 = (bf16[256,1024]{1,0:T(8,128)(2,1)}, bf16[256,1024]{1,0:T(8,128)(2,1)}, u32[]{:S(2)}, u32[]{:S(2)}) collective-permute-start(bf16[256,1024]{1,0:T(8,128)(2,1)} %copy-done.7), channel_id=1, source_target_pairs={{0,16},{16,0},{1,17},{17,1},{2,18},{18,2},{3,19},{19,3},{4,20},{20... | collective-permute-start | bytes 1572872 | tf_op jit(solution)/shard_map/ppermute | solution.py:472
  210.6 16.7 %collective-permute-start.53 = (bf16[256,1024]{1,0:T(8,128)(2,1)}, bf16[256,1024]{1,0:T(8,128)(2,1)}, u32[]{:S(2)}, u32[]{:S(2)}) collective-permute-start(bf16[256,1024]{1,0:T(8,128)(2,1)} %collective-permute-done.43.refs_0_), channel_id=1, source_target_pairs={{0,16},{16,0},{1,17},{17,1},{2,18},{18,2},{3,19},{19,3},{4,20},{20... | collective-permute-start | bytes 1572872 | tf_op jit(solution)/shard_map/ppermute | solution.py:472
  211.6 15.7 %collective-permute-start.54 = (bf16[256,1024]{1,0:T(8,128)(2,1)}, bf16[256,1024]{1,0:T(8,128)(2,1)}, u32[]{:S(2)}, u32[]{:S(2)}) collective-permute-start(bf16[256,1024]{1,0:T(8,128)(2,1)} %collective-permute-done.49.refs_1_), channel_id=1, source_target_pairs={{0,16},{16,0},{1,17},{17,1},{2,18},{18,2},{3,19},{19,3},{4,20},{20... | collective-permute-start | bytes 1572872 | tf_op jit(solution)/shard_map/ppermute | solution.py:472
  211.7 19.2 %collective-permute-start.51 = (bf16[256,1024]{1,0:T(8,128)(2,1)}, bf16[256,1024]{1,0:T(8,128)(2,1)}, u32[]{:S(2)}, u32[]{:S(2)}) collective-permute-start(bf16[256,1024]{1,0:T(8,128)(2,1)} %collective-permute-done.44.refs_0_), channel_id=1, source_target_pairs={{0,16},{16,0},{1,17},{17,1},{2,18},{18,2},{3,19},{19,3},{4,20},{20... | collective-permute-start | bytes 1572872 | tf_op jit(solution)/shard_map/ppermute | solution.py:472
  214.5 16.5 %collective-permute-start.52 = (bf16[256,1024]{1,0:T(8,128)(2,1)}, bf16[256,1024]{1,0:T(8,128)(2,1)}, u32[]{:S(2)}, u32[]{:S(2)}) collective-permute-start(bf16[256,1024]{1,0:T(8,128)(2,1)} %collective-permute-done.50.refs_1_), channel_id=1, source_target_pairs={{0,16},{16,0},{1,17},{17,1},{2,18},{18,2},{3,19},{19,3},{4,20},{20... | collective-permute-start | bytes 1572872 | tf_op jit(solution)/shard_map/ppermute | solution.py:472
  (75 other events, 856.5 us)

commit v2 on v1

--- a/solution.py
+++ b/solution.py
@@ -424,15 +424,15 @@
 
     flat_vision = vision.reshape(samples * rows, model)
     kv_here = width // head_dim
-    chunks = chunks_of(kv_here)
+    chunks = chunks_of()
     key_raw, kv_rel = project(me_ref, key_gain, flat_vision, key_weight, value_weight, samples, chunks)
     kv_blocks = []
     for c in range(chunks):
         pair = swap(kv_rel[1][c], 1)
         blocks = [kv_rel[0][c], pair] + [None] * (n - 2)
-        for z in range(n // 2 - 1, 0, -1):
-            blocks[2 * z] = swap(kv_rel[0][c], 2 * z)
-            blocks[2 * z + 1] = swap(pair, 2 * z)
+        for z, step in doubling(n // 2):
+            blocks[2 * z] = swap(blocks[2 * (z - step)], 2 * step)
+            blocks[2 * z + 1] = swap(blocks[2 * (z - step) + 1], 2 * step)
         kv_blocks.append(blocks)
 
     others = swap(jnp.concatenate([pick(queries, x + 1), pick(out_grad, x + 1)], axis=0), 1)
@@ -522,8 +522,19 @@
     return (query_grad, vision_grad, key_weight_grad, value_weight_grad)
 
 
-def chunks_of(kv_here):
-    return 2 if kv_here % 2 == 0 else 1
+def doubling(size):
+    found = [0]
+    step = size // 2
+    moves = []
+    while step:
+        moves += [(z + step, step) for z in found]
+        found += [z + step for z in found]
+        step //= 2
+    return moves
+
+
+def chunks_of():
+    return 1
 
 
 def solution(mesh):

time: 238 us -> 239 us (level)
  waiting for transfers between devices: 98.7 us -> 117 us
  starting transfers between devices: 69.5 us -> 54.2 us
  Pallas kernels: 50 us -> 47.4 us
    ppermute x26 -> x19, waiting for transfers between devices: 44.3 us -> 62 us  [swap(): return lax.ppermute(value, 'seq', [(i, i ^ j) for i in range(n)])]
    ppermute x26 -> x19, starting transfers between devices: 45.2 us -> 31.6 us  [swap(): return lax.ppermute(value, 'seq', [(i, i ^ j) for i in range(n)])]
    pallas_call x2 -> x1, Pallas kernels: 16.3 us -> 13.8 us  [attention(): pl.pallas_call(functools.partial(attention_kernel, blocks, parts, group,...]
    unnamed x84 -> x68, local copies, waits for them, and re-layouts: 4.44 us -> 5.43 us
  transfers between devices with their start and end apart: 57 -> 50, of which waited for: 23 -> 28; matrix products, arithmetic and copies ran while one was open for 4% -> 4% of each run, Pallas kernels for 13% -> 10%
where the time goes in v2:
time: 239 us; the launch traced here: 238 us
  waiting for transfers between devices  117 us (49%)
  starting transfers between devices  54.2 us (23%)
  Pallas kernels  47.4 us (20%)
  local copies, waits for them, and re-layouts  9.75 us (4%)
  matrix products  5.31 us (2%)
  other arithmetic  3.61 us (2%)
    ppermute x19, waiting for transfers between devices, swap(): return lax.ppermute(value, 'seq', [(i, i ^ j) for i in range(n)])  62 us
    ppermute x14, waiting for transfers between devices, split_ring(): return lax.ppermute(value, ('dp', 'seq'), perm)  49.4 us
    ppermute x19, starting transfers between devices, swap(): return lax.ppermute(value, 'seq', [(i, i ^ j) for i in range(n)])  31.6 us
    pallas_call x5, Pallas kernels, scatter_rows(): pl.pallas_call(functools.partial(scatter_kernel, pieces, n, share), in_sp...  16.1 us
    ppermute x14, starting transfers between devices, split_ring(): return lax.ppermute(value, ('dp', 'seq'), perm)  13.9 us
    pallas_call x1, Pallas kernels, attention(): pl.pallas_call(functools.partial(attention_kernel, blocks, parts, group,...  13.8 us
    pallas_call x1, Pallas kernels, project(): pl.pallas_call(functools.partial(project_kernel, samples, chunks, head_di...  8.35 us
    unnamed x68, local copies, waits for them, and re-layouts  5.43 us
  transfers between devices with their start and end apart: 50, of which 28 were waited for; matrix products, arithmetic and copies ran while one was open for 4% of the time, Pallas kernels for 10%

profile of v2, /device:TPU:0, one launch (start us, length us, event | category | flops | bytes accessed | tf_op | source)
XLA Modules:
  0.0 238.4 jit_solution(9206165250547049894)
XLA Ops:
  2.0 3.0 %collective-permute-start = (bf16[256,2048]{1,0:T(8,128)(2,1)S(1)}, bf16[256,2048]{1,0:T(8,128)(2,1)S(1)}, u32[]{:S(2)}, u32[]{:S(2)}) collective-permute-start(bf16[256,2048]{1,0:T(8,128)(2,1)S(1)} %pad_maximum_fusion), channel_id=1, source_target_pairs={{0,2},{2,0},{4,6},{6,4},{8,10},{10,8},{12,14},{14,12},{1,3},{3,1},... | collective-permute-start | bytes 3145736 | tf_op jit(solution)/shard_map/ppermute | solution.py:413
  5.1 8.3 %project.1 = (f32[160,512]{1,0:T(8,128)}, bf16[80,1024]{1,0:T(8,128)(2,1)}, bf16[80,1024]{1,0:T(8,128)(2,1)}) custom-call(s32[1]{0:T(128)} %bitcast.me_ref, f32[1,128]{1,0:T(1,128)} %bitcast.26, bf16[160,4096]{1,0:T(8,128)(2,1)} %bitcast.24, bf16[4096,512]{1,0:T(8,128)(2,1)} %key_ref.1, bf16[4096,512]{1,0:T(8,128)(2,1)} %value_ref.1), custom_call_target="tpu_custom_call" | custom-call | flops 1342177280 | bytes 9699328 | tf_op jit(solution)/shard_map/project/pallas_call | solution.py:188
  13.5 3.1 %collective-permute-start.4 = (bf16[80,1024]{1,0:T(8,128)(2,1)}, bf16[80,1024]{1,0:T(8,128)(2,1)S(1)}, u32[]{:S(2)}, u32[]{:S(2)}) collective-permute-start(bf16[80,1024]{1,0:T(8,128)(2,1)} %get-tuple-element.39.refs_4_), channel_id=1, source_target_pairs={{0,8},{2,10},{4,12},{6,14},{8,0},{10,2},{12,4},{14,6},{1,9},{3,11}... | collective-permute-start | bytes 491528 | tf_op jit(solution)/shard_map/ppermute | solution.py:413
  16.6 15.2 %collective-permute-done.1.refs_5_ = bf16[80,1024]{1,0:T(8,128)(2,1)S(1)} collective-permute-done((bf16[80,1024]{1,0:T(8,128)(2,1)}, bf16[80,1024]{1,0:T(8,128)(2,1)S(1)}, u32[]{:S(2)}, u32[]{:S(2)}) %collective-permute-start.1) | collective-permute-done | bytes 163872 | tf_op jit(solution)/shard_map/ppermute | solution.py:413
  38.2 3.3 %collective-permute-done.5.refs_9_ = bf16[80,1024]{1,0:T(8,128)(2,1)S(1)} collective-permute-done((bf16[80,1024]{1,0:T(8,128)(2,1)S(1)}, bf16[80,1024]{1,0:T(8,128)(2,1)S(1)}, u32[]{:S(2)}, u32[]{:S(2)}) %collective-permute-start.5) | collective-permute-done | bytes 163872 | tf_op jit(solution)/shard_map/ppermute | solution.py:413
  43.7 7.0 %collective-permute-done.6.refs_10_ = bf16[80,1024]{1,0:T(8,128)(2,1)S(1)} collective-permute-done((bf16[80,1024]{1,0:T(8,128)(2,1)S(1)}, bf16[80,1024]{1,0:T(8,128)(2,1)S(1)}, u32[]{:S(2)}, u32[]{:S(2)}) %collective-permute-start.6) | collective-permute-done | bytes 163872 | tf_op jit(solution)/shard_map/ppermute | solution.py:413
  53.6 13.8 %attention.1 = (bf16[2,128,2048]{2,1,0:T(8,128)(2,1)}, bf16[128,2048]{1,0:T(8,128)(2,1)}, bf16[80,1024]{1,0:T(8,128)(2,1)}, bf16[80,1024]{1,0:T(8,128)(2,1)}, bf...) custom-call(s32[1]{0:T(128)} %bitcast.me_ref, ...), custom_call_target="tpu_custom_call" | custom-call | flops 4026531840 | bytes 3145728 | tf_op jit(solution)/shard_map/attention/pallas_call | solution.py:120
  81.4 11.0 %collective-permute-done.18.refs_4_ = bf16[80,1024]{1,0:T(8,128)(2,1)S(1)} collective-permute-done((bf16[80,1024]{1,0:T(8,128)(2,1)}, bf16[80,1024]{1,0:T(8,128)(2,1)S(1)}, u32[]{:S(2)}, u32[]{:S(2)}) %collective-permute-start.18) | collective-permute-done | bytes 163872 | tf_op jit(solution)/shard_map/ppermute | solution.py:413
  92.4 4.5 %collective-permute-done.19.refs_5_ = bf16[80,1024]{1,0:T(8,128)(2,1)S(1)} collective-permute-done((bf16[80,1024]{1,0:T(8,128)(2,1)}, bf16[80,1024]{1,0:T(8,128)(2,1)S(1)}, u32[]{:S(2)}, u32[]{:S(2)}) %collective-permute-start.19) | collective-permute-done | bytes 163872 | tf_op jit(solution)/shard_map/ppermute | solution.py:413
  101.2 5.3 %collective-permute-start.10 = (bf16[80,1024]{1,0:T(8,128)(2,1)S(1)}, bf16[80,1024]{1,0:T(8,128)(2,1)S(1)}, u32[]{:S(2)}, u32[]{:S(2)}) collective-permute-start(bf16[80,1024]{1,0:T(8,128)(2,1)S(1)} %get-tuple-element.77), channel_id=1, source_target_pairs={{0,8},{2,10},{4,12},{6,14},{8,0},{10,2},{12,4},{14,6},{1,9},{3,11}... | collective-permute-start | bytes 491528 | tf_op jit(solution)/shard_map/ppermute | solution.py:413
  108.9 9.7 %collective-permute-done.10.refs_2_ = bf16[80,1024]{1,0:T(8,128)(2,1)S(1)} collective-permute-done((bf16[80,1024]{1,0:T(8,128)(2,1)S(1)}, bf16[80,1024]{1,0:T(8,128)(2,1)S(1)}, u32[]{:S(2)}, u32[]{:S(2)}) %collective-permute-start.10) | collective-permute-done | bytes 163872 | tf_op jit(solution)/shard_map/ppermute | solution.py:413
  128.3 3.3 %collective-permute-done.12.refs_1_ = bf16[320,512]{1,0:T(8,128)(2,1)S(1)} collective-permute-done((bf16[320,512]{1,0:T(8,128)(2,1)}, bf16[320,512]{1,0:T(8,128)(2,1)S(1)}, u32[]{:S(2)}, u32[]{:S(2)}) %collective-permute-start.12) | collective-permute-done | bytes 327712 | tf_op jit(solution)/shard_map/ppermute | solution.py:413
  138.4 3.8 %fusion = f32[160,4096]{1,0:T(8,128)S(1)} fusion(bf16[4096,512]{1,0:T(8,128)(2,1)} %value_ref.1, bf16[160,1024]{1,0:T(8,128)(2,1)} %own_grads.1.refs_4_), kind=kOutput, calls=%fused_computation.8 | convolution fusion | flops 671088640 | bytes 6979584 | tf_op jit(solution)/shard_map/dot_general | solution.py:489
  157.8 4.6 %weight_grads.1 = (f32[256,1024]{1,0:T(8,128)}, bf16[256,1024]{1,0:T(8,128)(2,1)}) custom-call(s32[3]{0:T(128)} %pad_add_fusion.where_ref, bf16[320,512]{1,0:T(8,128)(2,1)} %get-tuple-element.56.refs_0_, bf16[320,512]{1,0:T(8,128)(2,1)} %copy-done.18, bf16[320,512]{1,0:T(8,128)(2,1)} %copy-done.20, bf16[320,512]{1,0:T(8,128)(2,1)} %copy-done.21, ...), custom_call_target="tpu_custom_call" | custom-call | flops 1342177280 | bytes 3932160 | tf_op jit(solution)/shard_map/weight_grads/pallas_call | solution.py:324
  169.3 6.0 %collective-permute-done.35.refs_0_ = bf16[256,1024]{1,0:T(8,128)(2,1)S(1)} collective-permute-done((bf16[256,1024]{1,0:T(8,128)(2,1)S(1)}, bf16[256,1024]{1,0:T(8,128)(2,1)S(1)}, u32[]{:S(2)}, u32[]{:S(2)}) %collective-permute-start.35) | collective-permute-done | bytes 524320 | tf_op jit(solution)/shard_map/ppermute | solution.py:478
  177.4 5.2 %collective-permute-done.41.refs_1_ = bf16[256,1024]{1,0:T(8,128)(2,1)} collective-permute-done((bf16[256,1024]{1,0:T(8,128)(2,1)S(1)}, bf16[256,1024]{1,0:T(8,128)(2,1)}, u32[]{:S(2)}, u32[]{:S(2)}) %collective-permute-start.41) | collective-permute-done | bytes 524320 | tf_op jit(solution)/shard_map/ppermute | solution.py:478
  182.7 9.7 %collective-permute-done.36.refs_0_ = bf16[256,1024]{1,0:T(8,128)(2,1)} collective-permute-done((bf16[256,1024]{1,0:T(8,128)(2,1)S(1)}, bf16[256,1024]{1,0:T(8,128)(2,1)}, u32[]{:S(2)}, u32[]{:S(2)}) %collective-permute-start.36) | collective-permute-done | bytes 524320 | tf_op jit(solution)/shard_map/ppermute | solution.py:478
  194.8 3.1 %collective-permute-done.8 = bf16[128,2048]{1,0:T(8,128)(2,1)} collective-permute-done((bf16[128,2048]{1,0:T(8,128)(2,1)}, bf16[128,2048]{1,0:T(8,128)(2,1)}, u32[]{:S(2)}, u32[]{:S(2)}) %collective-permute-start.8) | collective-permute-done | bytes 524320 | tf_op jit(solution)/shard_map/ppermute | solution.py:420
  198.0 5.6 %collective-permute-done.42.refs_1_ = bf16[256,1024]{1,0:T(8,128)(2,1)} collective-permute-done((bf16[256,1024]{1,0:T(8,128)(2,1)}, bf16[256,1024]{1,0:T(8,128)(2,1)}, u32[]{:S(2)}, u32[]{:S(2)}) %collective-permute-start.42) | collective-permute-done | bytes 524320 | tf_op jit(solution)/shard_map/ppermute | solution.py:478
  203.6 5.6 %collective-permute-done.37.refs_0_ = bf16[256,1024]{1,0:T(8,128)(2,1)} collective-permute-done((bf16[256,1024]{1,0:T(8,128)(2,1)}, bf16[256,1024]{1,0:T(8,128)(2,1)}, u32[]{:S(2)}, u32[]{:S(2)}) %collective-permute-start.37) | collective-permute-done | bytes 524320 | tf_op jit(solution)/shard_map/ppermute | solution.py:478
  214.8 5.6 %collective-permute-done.38.refs_0_ = bf16[256,1024]{1,0:T(8,128)(2,1)} collective-permute-done((bf16[256,1024]{1,0:T(8,128)(2,1)}, bf16[256,1024]{1,0:T(8,128)(2,1)}, u32[]{:S(2)}, u32[]{:S(2)}) %collective-permute-start.38) | collective-permute-done | bytes 524320 | tf_op jit(solution)/shard_map/ppermute | solution.py:478
  224.0 3.6 %scatter_rows.6 = (f32[4096,512]{1,0:T(8,128)}, f32[4096,512]{1,0:T(8,128)}) custom-call(s32[2]{0:T(128)} %pad_add_fusion.1.where_ref, bf16[256,1024]{1,0:T(8,128)(2,1)} %copy-done.4, bf16[256,1024]{1,0:T(8,128)(2,1)} %collective-permute-done.41.refs_1_, ...), custom_call_target="tpu_custom_call", output_to_operand_aliasing={{0}: (5, {}), {1}: (6, {})} | custom-call | flops 1048576000 | bytes 6291456 | tf_op jit(solution)/shard_map/scatter_rows/pallas_call | solution.py:371
  227.7 3.6 %scatter_rows.7 = (f32[4096,512]{1,0:T(8,128)}, f32[4096,512]{1,0:T(8,128)}) custom-call(s32[2]{0:T(128)} %pad_add_fusion.1.where_ref, bf16[256,1024]{1,0:T(8,128)(2,1)} %collective-permute-done.36.refs_0_, bf16[256,1024]{1,0:T(8,128)(2,1)} %collective-permute-done.42.refs_1_, ...), custom_call_target="tpu_custom_call", output_to_operand_aliasing={{0}: (5, {}), {1}: (6, {})} | custom-call | flops 1048576000 | bytes 6291456 | tf_op jit(solution)/shard_map/scatter_rows/pallas_call | solution.py:371
  232.1 3.6 %scatter_rows.8 = (f32[4096,512]{1,0:T(8,128)}, f32[4096,512]{1,0:T(8,128)}) custom-call(s32[2]{0:T(128)} %pad_add_fusion.1.where_ref, bf16[256,1024]{1,0:T(8,128)(2,1)} %collective-permute-done.37.refs_0_, bf16[256,1024]{1,0:T(8,128)(2,1)} %collective-permute-done.43.refs_1_, ...), custom_call_target="tpu_custom_call", output_to_operand_aliasing={{0}: (5, {}), {1}: (6, {})} | custom-call | flops 1048576000 | bytes 6291456 | tf_op jit(solution)/shard_map/scatter_rows/pallas_call | solution.py:371
  (167 shorter events, 89.5 us)
Async XLA Ops:
  2.0 50.5 %collective-permute-start = (bf16[256,2048]{1,0:T(8,128)(2,1)S(1)}, bf16[256,2048]{1,0:T(8,128)(2,1)S(1)}, u32[]{:S(2)}, u32[]{:S(2)}) collective-permute-start(bf16[256,2048]{1,0:T(8,128)(2,1)S(1)} %pad_maximum_fusion), channel_id=1, source_target_pairs={{0,2},{2,0},{4,6},{6,4},{8,10},{10,8},{12,14},{14,12},{1,3},{3,1},... | collective-permute-start | bytes 3145736 | tf_op jit(solution)/shard_map/ppermute | solution.py:413
  13.4 18.3 %collective-permute-start.1 = (bf16[80,1024]{1,0:T(8,128)(2,1)}, bf16[80,1024]{1,0:T(8,128)(2,1)S(1)}, u32[]{:S(2)}, u32[]{:S(2)}) collective-permute-start(bf16[80,1024]{1,0:T(8,128)(2,1)} %get-tuple-element.40), channel_id=1, source_target_pairs={{0,2},{2,0},{4,6},{6,4},{8,10},{10,8},{12,14},{14,12},{1,3},{3,1},... | collective-permute-start | bytes 491528 | tf_op jit(solution)/shard_map/ppermute | solution.py:413
  13.5 23.2 %collective-permute-start.4 = (bf16[80,1024]{1,0:T(8,128)(2,1)}, bf16[80,1024]{1,0:T(8,128)(2,1)S(1)}, u32[]{:S(2)}, u32[]{:S(2)}) collective-permute-start(bf16[80,1024]{1,0:T(8,128)(2,1)} %get-tuple-element.39.refs_4_), channel_id=1, source_target_pairs={{0,8},{2,10},{4,12},{6,14},{8,0},{10,2},{12,4},{14,6},{1,9},{3,11}... | collective-permute-start | bytes 491528 | tf_op jit(solution)/shard_map/ppermute | solution.py:413
  70.9 21.5 %collective-permute-start.18 = (bf16[80,1024]{1,0:T(8,128)(2,1)}, bf16[80,1024]{1,0:T(8,128)(2,1)S(1)}, u32[]{:S(2)}, u32[]{:S(2)}) collective-permute-start(bf16[80,1024]{1,0:T(8,128)(2,1)} %get-tuple-element.50), channel_id=1, source_target_pairs={{0,8},{2,10},{4,12},{6,14},{8,0},{10,2},{12,4},{14,6},{1,9},{3,11}... | collective-permute-start | bytes 491528 | tf_op jit(solution)/shard_map/ppermute | solution.py:413
  72.0 24.9 %collective-permute-start.19 = (bf16[80,1024]{1,0:T(8,128)(2,1)}, bf16[80,1024]{1,0:T(8,128)(2,1)S(1)}, u32[]{:S(2)}, u32[]{:S(2)}) collective-permute-start(bf16[80,1024]{1,0:T(8,128)(2,1)} %get-tuple-element.51), channel_id=1, source_target_pairs={{0,10},{2,8},{4,14},{6,12},{8,2},{10,0},{12,6},{14,4},{1,11},{3,9}... | collective-permute-start | bytes 491528 | tf_op jit(solution)/shard_map/ppermute | solution.py:413
  74.7 22.2 %collective-permute-start.20 = (bf16[80,1024]{1,0:T(8,128)(2,1)}, bf16[80,1024]{1,0:T(8,128)(2,1)S(1)}, u32[]{:S(2)}, u32[]{:S(2)}) collective-permute-start(bf16[80,1024]{1,0:T(8,128)(2,1)} %get-tuple-element.52), channel_id=1, source_target_pairs={{0,12},{2,14},{4,8},{6,10},{8,4},{10,6},{12,0},{14,2},{1,13},{3,15... | collective-permute-start | bytes 491528 | tf_op jit(solution)/shard_map/ppermute | solution.py:413
  79.6 17.3 %collective-permute-start.21 = (bf16[80,1024]{1,0:T(8,128)(2,1)}, bf16[80,1024]{1,0:T(8,128)(2,1)S(1)}, u32[]{:S(2)}, u32[]{:S(2)}) collective-permute-start(bf16[80,1024]{1,0:T(8,128)(2,1)} %get-tuple-element.53), channel_id=1, source_target_pairs={{0,14},{2,12},{4,10},{6,8},{8,6},{10,4},{12,2},{14,0},{1,15},{3,13... | collective-permute-start | bytes 491528 | tf_op jit(solution)/shard_map/ppermute | solution.py:413
  100.2 25.7 %collective-permute-start.27 = (bf16[160,1024]{1,0:T(8,128)(2,1)}, bf16[160,1024]{1,0:T(8,128)(2,1)S(1)}, u32[]{:S(2)}, u32[]{:S(2)}) collective-permute-start(bf16[160,1024]{1,0:T(8,128)(2,1)} %own_grads.1.refs_4_), channel_id=1, source_target_pairs={{0,16},{16,0},{1,17},{17,1},{2,18},{18,2},{3,19},{19,3},{4,20},{20... | collective-permute-start | bytes 983048 | tf_op jit(solution)/shard_map/ppermute | solution.py:472
  101.2 17.4 %collective-permute-start.10 = (bf16[80,1024]{1,0:T(8,128)(2,1)S(1)}, bf16[80,1024]{1,0:T(8,128)(2,1)S(1)}, u32[]{:S(2)}, u32[]{:S(2)}) collective-permute-start(bf16[80,1024]{1,0:T(8,128)(2,1)S(1)} %get-tuple-element.77), channel_id=1, source_target_pairs={{0,8},{2,10},{4,12},{6,14},{8,0},{10,2},{12,4},{14,6},{1,9},{3,11}... | collective-permute-start | bytes 491528 | tf_op jit(solution)/shard_map/ppermute | solution.py:413
  126.8 22.0 %collective-permute-start.13 = (bf16[320,512]{1,0:T(8,128)(2,1)}, bf16[320,512]{1,0:T(8,128)(2,1)S(1)}, u32[]{:S(2)}, u32[]{:S(2)}) collective-permute-start(bf16[320,512]{1,0:T(8,128)(2,1)} %get-tuple-element.56.refs_0_), channel_id=1, source_target_pairs={{0,1},{1,0},{2,3},{3,2},{4,5},{5,4},{6,7},{7,6},{8,9},{9,8},{10,11... | collective-permute-start | bytes 983048 | tf_op jit(solution)/shard_map/ppermute | solution.py:420
  131.5 21.5 %collective-permute-start.14 = (bf16[320,512]{1,0:T(8,128)(2,1)S(1)}, bf16[320,512]{1,0:T(8,128)(2,1)S(1)}, u32[]{:S(2)}, u32[]{:S(2)}) collective-permute-start(bf16[320,512]{1,0:T(8,128)(2,1)S(1)} %collective-permute-done.12.refs_1_), channel_id=1, source_target_pairs={{0,1},{1,0},{2,3},{3,2},{4,5},{5,4},{6,7},{7,6},{8,9},{9,8},{10,11... | collective-permute-start | bytes 983048 | tf_op jit(solution)/shard_map/ppermute | solution.py:420
  168.0 14.7 %collective-permute-start.41 = (bf16[256,1024]{1,0:T(8,128)(2,1)S(1)}, bf16[256,1024]{1,0:T(8,128)(2,1)}, u32[]{:S(2)}, u32[]{:S(2)}) collective-permute-start(bf16[256,1024]{1,0:T(8,128)(2,1)S(1)} %collective-permute-done.40.refs_1_), channel_id=1, source_target_pairs={{0,4},{4,8},{8,12},{12,14},{14,10},{10,6},{6,2},{2,0},{16,18},{20,... | collective-permute-start | bytes 1572872 | tf_op jit(solution)/shard_map/ppermute | solution.py:478
  175.4 17.0 %collective-permute-start.36 = (bf16[256,1024]{1,0:T(8,128)(2,1)S(1)}, bf16[256,1024]{1,0:T(8,128)(2,1)}, u32[]{:S(2)}, u32[]{:S(2)}) collective-permute-start(bf16[256,1024]{1,0:T(8,128)(2,1)S(1)} %collective-permute-done.35.refs_0_), channel_id=1, source_target_pairs={{0,4},{4,8},{8,12},{12,14},{14,10},{10,6},{6,2},{2,0},{16,18},{20,... | collective-permute-start | bytes 1572872 | tf_op jit(solution)/shard_map/ppermute | solution.py:478
  176.7 21.2 %collective-permute-start.8 = (bf16[128,2048]{1,0:T(8,128)(2,1)}, bf16[128,2048]{1,0:T(8,128)(2,1)}, u32[]{:S(2)}, u32[]{:S(2)}) collective-permute-start(bf16[128,2048]{1,0:T(8,128)(2,1)} %get-tuple-element.42), channel_id=1, source_target_pairs={{0,2},{2,0},{4,6},{6,4},{8,10},{10,8},{12,14},{14,12},{1,3},{3,1},... | collective-permute-start | bytes 1572872 | tf_op jit(solution)/shard_map/ppermute | solution.py:420
  182.6 20.9 %collective-permute-start.42 = (bf16[256,1024]{1,0:T(8,128)(2,1)}, bf16[256,1024]{1,0:T(8,128)(2,1)}, u32[]{:S(2)}, u32[]{:S(2)}) collective-permute-start(bf16[256,1024]{1,0:T(8,128)(2,1)} %collective-permute-done.41.refs_1_), channel_id=1, source_target_pairs={{0,4},{4,8},{8,12},{12,14},{14,10},{10,6},{6,2},{2,0},{16,18},{20,... | collective-permute-start | bytes 1572872 | tf_op jit(solution)/shard_map/ppermute | solution.py:478
  192.3 16.9 %collective-permute-start.37 = (bf16[256,1024]{1,0:T(8,128)(2,1)}, bf16[256,1024]{1,0:T(8,128)(2,1)}, u32[]{:S(2)}, u32[]{:S(2)}) collective-permute-start(bf16[256,1024]{1,0:T(8,128)(2,1)} %collective-permute-done.36.refs_0_), channel_id=1, source_target_pairs={{0,4},{4,8},{8,12},{12,14},{14,10},{10,6},{6,2},{2,0},{16,18},{20,... | collective-permute-start | bytes 1572872 | tf_op jit(solution)/shard_map/ppermute | solution.py:478
  192.3 19.4 %collective-permute-start.22 = (bf16[160,2048]{1,0:T(8,128)(2,1)S(1)}, bf16[160,2048]{1,0:T(8,128)(2,1)S(1)}, u32[]{:S(2)}, u32[]{:S(2)}) collective-permute-start(bf16[160,2048]{1,0:T(8,128)(2,1)S(1)} %dynamic-slice_convert_fusion), channel_id=1, source_target_pairs={{0,1},{1,0},{2,3},{3,2},{4,5},{5,4},{6,7},{7,6},{8,9},{9,8},{10,11... | collective-permute-start | bytes 1966088 | tf_op jit(solution)/shard_map/ppermute | solution.py:496
  193.9 19.0 %collective-permute-start.48 = (bf16[256,1024]{1,0:T(8,128)(2,1)}, bf16[256,1024]{1,0:T(8,128)(2,1)}, u32[]{:S(2)}, u32[]{:S(2)}) collective-permute-start(bf16[256,1024]{1,0:T(8,128)(2,1)} %copy-done.4), channel_id=1, source_target_pairs={{0,16},{16,0},{1,17},{17,1},{2,18},{18,2},{3,19},{19,3},{4,20},{20... | collective-permute-start | bytes 1572872 | tf_op jit(solution)/shard_map/ppermute | solution.py:472
  198.0 15.1 %collective-permute-start.49 = (bf16[256,1024]{1,0:T(8,128)(2,1)}, bf16[256,1024]{1,0:T(8,128)(2,1)}, u32[]{:S(2)}, u32[]{:S(2)}) collective-permute-start(bf16[256,1024]{1,0:T(8,128)(2,1)} %collective-permute-done.41.refs_1_), channel_id=1, source_target_pairs={{0,16},{16,0},{1,17},{17,1},{2,18},{18,2},{3,19},{19,3},{4,20},{20... | collective-permute-start | bytes 1572872 | tf_op jit(solution)/shard_map/ppermute | solution.py:472
  211.7 15.9 %collective-permute-start.46 = (bf16[256,1024]{1,0:T(8,128)(2,1)}, bf16[256,1024]{1,0:T(8,128)(2,1)}, u32[]{:S(2)}, u32[]{:S(2)}) collective-permute-start(bf16[256,1024]{1,0:T(8,128)(2,1)} %collective-permute-done.36.refs_0_), channel_id=1, source_target_pairs={{0,16},{16,0},{1,17},{17,1},{2,18},{18,2},{3,19},{19,3},{4,20},{20... | collective-permute-start | bytes 1572872 | tf_op jit(solution)/shard_map/ppermute | solution.py:472
  213.0 14.7 %collective-permute-start.47 = (bf16[256,1024]{1,0:T(8,128)(2,1)}, bf16[256,1024]{1,0:T(8,128)(2,1)}, u32[]{:S(2)}, u32[]{:S(2)}) collective-permute-start(bf16[256,1024]{1,0:T(8,128)(2,1)} %collective-permute-done.42.refs_1_), channel_id=1, source_target_pairs={{0,16},{16,0},{1,17},{17,1},{2,18},{18,2},{3,19},{19,3},{4,20},{20... | collective-permute-start | bytes 1572872 | tf_op jit(solution)/shard_map/ppermute | solution.py:472
  213.0 18.3 %collective-permute-start.44 = (bf16[256,1024]{1,0:T(8,128)(2,1)}, bf16[256,1024]{1,0:T(8,128)(2,1)S(1)}, u32[]{:S(2)}, u32[]{:S(2)}) collective-permute-start(bf16[256,1024]{1,0:T(8,128)(2,1)} %collective-permute-done.37.refs_0_), channel_id=1, source_target_pairs={{0,16},{16,0},{1,17},{17,1},{2,18},{18,2},{3,19},{19,3},{4,20},{20... | collective-permute-start | bytes 1572872 | tf_op jit(solution)/shard_map/ppermute | solution.py:472
  214.8 16.5 %collective-permute-start.45 = (bf16[256,1024]{1,0:T(8,128)(2,1)}, bf16[256,1024]{1,0:T(8,128)(2,1)}, u32[]{:S(2)}, u32[]{:S(2)}) collective-permute-start(bf16[256,1024]{1,0:T(8,128)(2,1)} %collective-permute-done.43.refs_1_), channel_id=1, source_target_pairs={{0,16},{16,0},{1,17},{17,1},{2,18},{18,2},{3,19},{19,3},{4,20},{20... | collective-permute-start | bytes 1572872 | tf_op jit(solution)/shard_map/ppermute | solution.py:472
  220.4 15.3 %collective-permute-start.39 = (bf16[256,1024]{1,0:T(8,128)(2,1)}, bf16[256,1024]{1,0:T(8,128)(2,1)}, u32[]{:S(2)}, u32[]{:S(2)}) collective-permute-start(bf16[256,1024]{1,0:T(8,128)(2,1)} %collective-permute-done.38.refs_0_), channel_id=1, source_target_pairs={{0,16},{16,0},{1,17},{17,1},{2,18},{18,2},{3,19},{19,3},{4,20},{20... | collective-permute-start | bytes 1572872 | tf_op jit(solution)/shard_map/ppermute | solution.py:472
  (60 other events, 625.2 us)

commit v3 on v2

--- a/solution.py
+++ b/solution.py
@@ -183,7 +183,7 @@
     width = key_weight.shape[1]
     head_dim = gain.shape[0]
     rows = all_rows // samples
-    step = math.gcd(model, 512)
+    step = math.gcd(model, 2048)
     weight = pl.BlockSpec((step, width), lambda i, m: (i, 0))
     results = pl.pallas_call(
         functools.partial(project_kernel, samples, chunks, head_dim),
@@ -480,7 +480,8 @@
     grads = [own_grads] + [None] * (n - 1)
     held = [own_grads, across(own_grads)]
     for k in range(1, n // 2):
-        held = [split_ring(v) for v in held]
+        for core in range(dps):
+            held[core] = split_ring(held[core])
         grads[k], grads[n - k] = held[0], across(held[1])
     grads[n // 2] = split_ring(held[0])
 
@@ -490,7 +491,6 @@
     cols = model // mps
     slices = [lax.dynamic_slice_in_dim(full, (mp + k) % mps * cols, cols, axis=1) for k in range(mps)]
     slices = [slices[0]] + [v.astype(BF16) for v in slices[1:]]
-    vision_rows, slices = lax.optimization_barrier((vision_rows, slices))
     received = []
     for k in range(1, mps):
         received.append(lax.ppermute(slices[k], "mp", [(i, (i + k) % mps) for i in range(mps)]))

time: 239 us -> 238 us (level)
  starting transfers between devices: 54.2 us -> 60.6 us
  waiting for transfers between devices: 117 us -> 113 us
  Pallas kernels: 47.4 us -> 44.9 us
    ppermute x14, waiting for transfers between devices: 49.4 us -> 43.9 us  [split_ring(): return lax.ppermute(value, ('dp', 'seq'), perm)]
    ppermute x14, starting transfers between devices: 13.9 us -> 18.6 us  [split_ring(): return lax.ppermute(value, ('dp', 'seq'), perm)]
    ppermute x19, starting transfers between devices: 31.6 us -> 34.3 us  [swap(): return lax.ppermute(value, 'seq', [(i, i ^ j) for i in range(n)])]
    pallas_call x1, Pallas kernels: 8.35 us -> 5.79 us  [project(): pl.pallas_call(functools.partial(project_kernel, samples, chunks, head_di...]
    unnamed x68 -> x66, local copies, waits for them, and re-layouts: 5.43 us -> 3.93 us
  transfers between devices with their start and end apart: 50 -> 50, of which waited for: 28 -> 29; matrix products, arithmetic and copies ran while one was open for 4% -> 5% of each run, Pallas kernels for 10% -> 9%
where the time goes in v3:
time: 238 us; the launch traced here: 237 us
  waiting for transfers between devices  113 us (47%)
  starting transfers between devices  60.6 us (25%)
  Pallas kernels  44.9 us (19%)
  local copies, waits for them, and re-layouts  9 us (4%)
  matrix products  5.21 us (2%)
  other arithmetic  3.6 us (2%)
    ppermute x19, waiting for transfers between devices, swap(): return lax.ppermute(value, 'seq', [(i, i ^ j) for i in range(n)])  61.4 us
    ppermute x14, waiting for transfers between devices, split_ring(): return lax.ppermute(value, ('dp', 'seq'), perm)  43.9 us
    ppermute x19, starting transfers between devices, swap(): return lax.ppermute(value, 'seq', [(i, i ^ j) for i in range(n)])  34.3 us
    ppermute x14, starting transfers between devices, split_ring(): return lax.ppermute(value, ('dp', 'seq'), perm)  18.6 us
    pallas_call x5, Pallas kernels, scatter_rows(): pl.pallas_call(functools.partial(scatter_kernel, pieces, n, share), in_sp...  16.1 us
    pallas_call x1, Pallas kernels, attention(): pl.pallas_call(functools.partial(attention_kernel, blocks, parts, group,...  13.8 us
    pallas_call x1, Pallas kernels, project(): pl.pallas_call(functools.partial(project_kernel, samples, chunks, head_di...  5.79 us
  transfers between devices with their start and end apart: 50, of which 29 were waited for; matrix products, arithmetic and copies ran while one was open for 5% of the time, Pallas kernels for 9%

profile of v3, /device:TPU:0, one launch (start us, length us, event | category | flops | bytes accessed | tf_op | source)
XLA Modules:
  0.0 237.0 jit_solution(9167280511293170322)
XLA Ops:
  5.1 5.8 %project.1 = (f32[160,512]{1,0:T(8,128)}, bf16[80,1024]{1,0:T(8,128)(2,1)}, bf16[80,1024]{1,0:T(8,128)(2,1)}) custom-call(s32[1]{0:T(128)} %bitcast.me_ref, f32[1,128]{1,0:T(1,128)} %bitcast.26, bf16[160,4096]{1,0:T(8,128)(2,1)} %bitcast.24, bf16[4096,512]{1,0:T(8,128)(2,1)} %key_ref.1, bf16[4096,512]{1,0:T(8,128)(2,1)} %value_ref.1), custom_call_target="tpu_custom_call" | custom-call | flops 1342177280 | bytes 9699328 | tf_op jit(solution)/shard_map/project/pallas_call | solution.py:188
  10.9 3.1 %collective-permute-start.4 = (bf16[80,1024]{1,0:T(8,128)(2,1)}, bf16[80,1024]{1,0:T(8,128)(2,1)S(1)}, u32[]{:S(2)}, u32[]{:S(2)}) collective-permute-start(bf16[80,1024]{1,0:T(8,128)(2,1)} %get-tuple-element.33.refs_4_), channel_id=1, source_target_pairs={{0,8},{2,10},{4,12},{6,14},{8,0},{10,2},{12,4},{14,6},{1,9},{3,11}... | collective-permute-start | bytes 491528 | tf_op jit(solution)/shard_map/ppermute | solution.py:413
  14.0 17.8 %collective-permute-done.1.refs_5_ = bf16[80,1024]{1,0:T(8,128)(2,1)S(1)} collective-permute-done((bf16[80,1024]{1,0:T(8,128)(2,1)}, bf16[80,1024]{1,0:T(8,128)(2,1)S(1)}, u32[]{:S(2)}, u32[]{:S(2)}) %collective-permute-start.1) | collective-permute-done | bytes 163872 | tf_op jit(solution)/shard_map/ppermute | solution.py:413
  38.2 3.3 %collective-permute-done.5.refs_9_ = bf16[80,1024]{1,0:T(8,128)(2,1)S(1)} collective-permute-done((bf16[80,1024]{1,0:T(8,128)(2,1)S(1)}, bf16[80,1024]{1,0:T(8,128)(2,1)S(1)}, u32[]{:S(2)}, u32[]{:S(2)}) %collective-permute-start.5) | collective-permute-done | bytes 163872 | tf_op jit(solution)/shard_map/ppermute | solution.py:413
  43.7 7.0 %collective-permute-done.6.refs_10_ = bf16[80,1024]{1,0:T(8,128)(2,1)S(1)} collective-permute-done((bf16[80,1024]{1,0:T(8,128)(2,1)S(1)}, bf16[80,1024]{1,0:T(8,128)(2,1)S(1)}, u32[]{:S(2)}, u32[]{:S(2)}) %collective-permute-start.6) | collective-permute-done | bytes 163872 | tf_op jit(solution)/shard_map/ppermute | solution.py:413
  53.6 13.8 %attention.1 = (bf16[2,128,2048]{2,1,0:T(8,128)(2,1)}, bf16[128,2048]{1,0:T(8,128)(2,1)}, bf16[80,1024]{1,0:T(8,128)(2,1)}, bf16[80,1024]{1,0:T(8,128)(2,1)}, bf...) custom-call(s32[1]{0:T(128)} %bitcast.me_ref, ...), custom_call_target="tpu_custom_call" | custom-call | flops 4026531840 | bytes 3145728 | tf_op jit(solution)/shard_map/attention/pallas_call | solution.py:120
  78.2 3.0 %collective-permute-start.15 = (bf16[80,1024]{1,0:T(8,128)(2,1)}, bf16[80,1024]{1,0:T(8,128)(2,1)S(1)}, u32[]{:S(2)}, u32[]{:S(2)}) collective-permute-start(bf16[80,1024]{1,0:T(8,128)(2,1)} %get-tuple-element.45), channel_id=1, source_target_pairs={{0,14},{2,12},{4,10},{6,8},{8,6},{10,4},{12,2},{14,0},{1,15},{3,13... | collective-permute-start | bytes 491528 | tf_op jit(solution)/shard_map/ppermute | solution.py:413
  81.6 10.6 %collective-permute-done.12.refs_4_ = bf16[80,1024]{1,0:T(8,128)(2,1)S(1)} collective-permute-done((bf16[80,1024]{1,0:T(8,128)(2,1)}, bf16[80,1024]{1,0:T(8,128)(2,1)S(1)}, u32[]{:S(2)}, u32[]{:S(2)}) %collective-permute-start.12) | collective-permute-done | bytes 163872 | tf_op jit(solution)/shard_map/ppermute | solution.py:413
  92.2 3.4 %collective-permute-done.13.refs_5_ = bf16[80,1024]{1,0:T(8,128)(2,1)S(1)} collective-permute-done((bf16[80,1024]{1,0:T(8,128)(2,1)}, bf16[80,1024]{1,0:T(8,128)(2,1)S(1)}, u32[]{:S(2)}, u32[]{:S(2)}) %collective-permute-start.13) | collective-permute-done | bytes 163872 | tf_op jit(solution)/shard_map/ppermute | solution.py:413
  99.0 4.9 %collective-permute-start.23 = (bf16[160,1024]{1,0:T(8,128)(2,1)}, bf16[160,1024]{1,0:T(8,128)(2,1)S(1)}, u32[]{:S(2)}, u32[]{:S(2)}) collective-permute-start(bf16[160,1024]{1,0:T(8,128)(2,1)} %own_grads.1.refs_4_), channel_id=1, source_target_pairs={{0,4},{4,8},{8,12},{12,14},{14,10},{10,6},{6,2},{2,0},{16,18},{20,... | collective-permute-start | bytes 983048 | tf_op jit(solution)/shard_map/ppermute | solution.py:478
  105.7 3.1 %collective-permute-done.23.refs_5_ = bf16[160,1024]{1,0:T(8,128)(2,1)S(1)} collective-permute-done((bf16[160,1024]{1,0:T(8,128)(2,1)}, bf16[160,1024]{1,0:T(8,128)(2,1)S(1)}, u32[]{:S(2)}, u32[]{:S(2)}) %collective-permute-start.23) | collective-permute-done | bytes 327712 | tf_op jit(solution)/shard_map/ppermute | solution.py:478
  120.6 5.7 %collective-permute-done.17.refs_1_ = bf16[80,1024]{1,0:T(8,128)(2,1)S(1)} collective-permute-done((bf16[80,1024]{1,0:T(8,128)(2,1)S(1)}, bf16[80,1024]{1,0:T(8,128)(2,1)S(1)}, u32[]{:S(2)}, u32[]{:S(2)}) %collective-permute-start.17) | collective-permute-done | bytes 163872 | tf_op jit(solution)/shard_map/ppermute | solution.py:413
  132.6 5.1 %collective-permute-start.20 = (bf16[320,512]{1,0:T(8,128)(2,1)}, bf16[320,512]{1,0:T(8,128)(2,1)S(1)}, u32[]{:S(2)}, u32[]{:S(2)}) collective-permute-start(bf16[320,512]{1,0:T(8,128)(2,1)} %get-tuple-element.47), channel_id=1, source_target_pairs={{0,2},{2,0},{4,6},{6,4},{8,10},{10,8},{12,14},{14,12},{1,3},{3,1},... | collective-permute-start | bytes 983048 | tf_op jit(solution)/shard_map/ppermute | solution.py:413
  142.1 4.0 %collective-permute-done.20.refs_1_ = bf16[320,512]{1,0:T(8,128)(2,1)S(1)} collective-permute-done((bf16[320,512]{1,0:T(8,128)(2,1)}, bf16[320,512]{1,0:T(8,128)(2,1)S(1)}, u32[]{:S(2)}, u32[]{:S(2)}) %collective-permute-start.20) | collective-permute-done | bytes 327712 | tf_op jit(solution)/shard_map/ppermute | solution.py:413
  157.1 4.6 %weight_grads.1 = (f32[256,1024]{1,0:T(8,128)}, bf16[256,1024]{1,0:T(8,128)(2,1)}) custom-call(s32[3]{0:T(128)} %pad_add_fusion.1.where_ref, bf16[320,512]{1,0:T(8,128)(2,1)} %get-tuple-element.46.refs_0_, bf16[320,512]{1,0:T(8,128)(2,1)} %copy-done.19, bf16[320,512]{1,0:T(8,128)(2,1)} %copy-done.20, bf16[320,512]{1,0:T(8,128)(2,1)} %copy-done.22, ...), custom_call_target="tpu_custom_call" | custom-call | flops 1342177280 | bytes 3932160 | tf_op jit(solution)/shard_map/weight_grads/pallas_call | solution.py:324
  168.1 6.6 %collective-permute-done.35.refs_0_ = bf16[256,1024]{1,0:T(8,128)(2,1)S(1)} collective-permute-done((bf16[256,1024]{1,0:T(8,128)(2,1)S(1)}, bf16[256,1024]{1,0:T(8,128)(2,1)S(1)}, u32[]{:S(2)}, u32[]{:S(2)}) %collective-permute-start.35) | collective-permute-done | bytes 524320 | tf_op jit(solution)/shard_map/ppermute | solution.py:478
  176.8 3.7 %fusion = f32[160,4096]{1,0:T(8,128)S(1)} fusion(bf16[4096,512]{1,0:T(8,128)(2,1)} %value_ref.1, bf16[160,1024]{1,0:T(8,128)(2,1)S(1)} %copy-done.3), kind=kOutput, calls=%fused_computation.8 | convolution fusion | flops 671088640 | bytes 6979584 | tf_op jit(solution)/shard_map/dot_general | solution.py:490
  182.5 9.1 %collective-permute-done.36.refs_0_ = bf16[256,1024]{1,0:T(8,128)(2,1)} collective-permute-done((bf16[256,1024]{1,0:T(8,128)(2,1)S(1)}, bf16[256,1024]{1,0:T(8,128)(2,1)}, u32[]{:S(2)}, u32[]{:S(2)}) %collective-permute-start.36) | collective-permute-done | bytes 524320 | tf_op jit(solution)/shard_map/ppermute | solution.py:478
  197.3 5.6 %collective-permute-done.42.refs_1_ = bf16[256,1024]{1,0:T(8,128)(2,1)} collective-permute-done((bf16[256,1024]{1,0:T(8,128)(2,1)}, bf16[256,1024]{1,0:T(8,128)(2,1)}, u32[]{:S(2)}, u32[]{:S(2)}) %collective-permute-start.42) | collective-permute-done | bytes 524320 | tf_op jit(solution)/shard_map/ppermute | solution.py:478
  202.9 5.6 %collective-permute-done.37.refs_0_ = bf16[256,1024]{1,0:T(8,128)(2,1)} collective-permute-done((bf16[256,1024]{1,0:T(8,128)(2,1)}, bf16[256,1024]{1,0:T(8,128)(2,1)}, u32[]{:S(2)}, u32[]{:S(2)}) %collective-permute-start.37) | collective-permute-done | bytes 524320 | tf_op jit(solution)/shard_map/ppermute | solution.py:478
  214.1 5.6 %collective-permute-done.38.refs_0_ = bf16[256,1024]{1,0:T(8,128)(2,1)} collective-permute-done((bf16[256,1024]{1,0:T(8,128)(2,1)}, bf16[256,1024]{1,0:T(8,128)(2,1)}, u32[]{:S(2)}, u32[]{:S(2)}) %collective-permute-start.38) | collective-permute-done | bytes 524320 | tf_op jit(solution)/shard_map/ppermute | solution.py:478
  223.3 3.6 %scatter_rows.6 = (f32[4096,512]{1,0:T(8,128)}, f32[4096,512]{1,0:T(8,128)}) custom-call(s32[2]{0:T(128)} %pad_add_fusion.where_ref, bf16[256,1024]{1,0:T(8,128)(2,1)} %copy-done.4, bf16[256,1024]{1,0:T(8,128)(2,1)} %collective-permute-done.41.refs_1_, ...), custom_call_target="tpu_custom_call", output_to_operand_aliasing={{0}: (5, {}), {1}: (6, {})} | custom-call | flops 1048576000 | bytes 6291456 | tf_op jit(solution)/shard_map/scatter_rows/pallas_call | solution.py:371
  227.0 3.6 %scatter_rows.7 = (f32[4096,512]{1,0:T(8,128)}, f32[4096,512]{1,0:T(8,128)}) custom-call(s32[2]{0:T(128)} %pad_add_fusion.where_ref, bf16[256,1024]{1,0:T(8,128)(2,1)} %collective-permute-done.36.refs_0_, bf16[256,1024]{1,0:T(8,128)(2,1)} %collective-permute-done.42.refs_1_, ...), custom_call_target="tpu_custom_call", output_to_operand_aliasing={{0}: (5, {}), {1}: (6, {})} | custom-call | flops 1048576000 | bytes 6291456 | tf_op jit(solution)/shard_map/scatter_rows/pallas_call | solution.py:371
  230.6 3.6 %scatter_rows.8 = (f32[4096,512]{1,0:T(8,128)}, f32[4096,512]{1,0:T(8,128)}) custom-call(s32[2]{0:T(128)} %pad_add_fusion.where_ref, bf16[256,1024]{1,0:T(8,128)(2,1)} %collective-permute-done.37.refs_0_, bf16[256,1024]{1,0:T(8,128)(2,1)} %collective-permute-done.43.refs_1_, ...), custom_call_target="tpu_custom_call", output_to_operand_aliasing={{0}: (5, {}), {1}: (6, {})} | custom-call | flops 1048576000 | bytes 6291456 | tf_op jit(solution)/shard_map/scatter_rows/pallas_call | solution.py:371
  (164 shorter events, 93.5 us)
Async XLA Ops:
  2.0 50.5 %collective-permute-start = (bf16[256,2048]{1,0:T(8,128)(2,1)S(1)}, bf16[256,2048]{1,0:T(8,128)(2,1)S(1)}, u32[]{:S(2)}, u32[]{:S(2)}) collective-permute-start(bf16[256,2048]{1,0:T(8,128)(2,1)S(1)} %pad_maximum_fusion), channel_id=1, source_target_pairs={{0,2},{2,0},{4,6},{6,4},{8,10},{10,8},{12,14},{14,12},{1,3},{3,1},... | collective-permute-start | bytes 3145736 | tf_op jit(solution)/shard_map/ppermute | solution.py:413
  10.9 20.9 %collective-permute-start.1 = (bf16[80,1024]{1,0:T(8,128)(2,1)}, bf16[80,1024]{1,0:T(8,128)(2,1)S(1)}, u32[]{:S(2)}, u32[]{:S(2)}) collective-permute-start(bf16[80,1024]{1,0:T(8,128)(2,1)} %get-tuple-element.34), channel_id=1, source_target_pairs={{0,2},{2,0},{4,6},{6,4},{8,10},{10,8},{12,14},{14,12},{1,3},{3,1},... | collective-permute-start | bytes 491528 | tf_op jit(solution)/shard_map/ppermute | solution.py:413
  10.9 25.7 %collective-permute-start.4 = (bf16[80,1024]{1,0:T(8,128)(2,1)}, bf16[80,1024]{1,0:T(8,128)(2,1)S(1)}, u32[]{:S(2)}, u32[]{:S(2)}) collective-permute-start(bf16[80,1024]{1,0:T(8,128)(2,1)} %get-tuple-element.33.refs_4_), channel_id=1, source_target_pairs={{0,8},{2,10},{4,12},{6,14},{8,0},{10,2},{12,4},{14,6},{1,9},{3,11}... | collective-permute-start | bytes 491528 | tf_op jit(solution)/shard_map/ppermute | solution.py:413
  36.2 14.6 %collective-permute-start.3 = (bf16[80,1024]{1,0:T(8,128)(2,1)S(1)}, bf16[80,1024]{1,0:T(8,128)(2,1)S(1)}, u32[]{:S(2)}, u32[]{:S(2)}) collective-permute-start(bf16[80,1024]{1,0:T(8,128)(2,1)S(1)} %collective-permute-done.1.refs_5_), channel_id=1, source_target_pairs={{0,4},{2,6},{4,0},{6,2},{8,12},{10,14},{12,8},{14,10},{1,5},{3,7},... | collective-permute-start | bytes 491528 | tf_op jit(solution)/shard_map/ppermute | solution.py:413
  70.3 21.9 %collective-permute-start.12 = (bf16[80,1024]{1,0:T(8,128)(2,1)}, bf16[80,1024]{1,0:T(8,128)(2,1)S(1)}, u32[]{:S(2)}, u32[]{:S(2)}) collective-permute-start(bf16[80,1024]{1,0:T(8,128)(2,1)} %get-tuple-element.42), channel_id=1, source_target_pairs={{0,8},{2,10},{4,12},{6,14},{8,0},{10,2},{12,4},{14,6},{1,9},{3,11}... | collective-permute-start | bytes 491528 | tf_op jit(solution)/shard_map/ppermute | solution.py:413
  71.5 24.1 %collective-permute-start.13 = (bf16[80,1024]{1,0:T(8,128)(2,1)}, bf16[80,1024]{1,0:T(8,128)(2,1)S(1)}, u32[]{:S(2)}, u32[]{:S(2)}) collective-permute-start(bf16[80,1024]{1,0:T(8,128)(2,1)} %get-tuple-element.43), channel_id=1, source_target_pairs={{0,10},{2,8},{4,14},{6,12},{8,2},{10,0},{12,6},{14,4},{1,11},{3,9}... | collective-permute-start | bytes 491528 | tf_op jit(solution)/shard_map/ppermute | solution.py:413
  73.3 22.3 %collective-permute-start.14 = (bf16[80,1024]{1,0:T(8,128)(2,1)}, bf16[80,1024]{1,0:T(8,128)(2,1)S(1)}, u32[]{:S(2)}, u32[]{:S(2)}) collective-permute-start(bf16[80,1024]{1,0:T(8,128)(2,1)} %get-tuple-element.44), channel_id=1, source_target_pairs={{0,12},{2,14},{4,8},{6,10},{8,4},{10,6},{12,0},{14,2},{1,13},{3,15... | collective-permute-start | bytes 491528 | tf_op jit(solution)/shard_map/ppermute | solution.py:413
  78.2 17.4 %collective-permute-start.15 = (bf16[80,1024]{1,0:T(8,128)(2,1)}, bf16[80,1024]{1,0:T(8,128)(2,1)S(1)}, u32[]{:S(2)}, u32[]{:S(2)}) collective-permute-start(bf16[80,1024]{1,0:T(8,128)(2,1)} %get-tuple-element.45), channel_id=1, source_target_pairs={{0,14},{2,12},{4,10},{6,8},{8,6},{10,4},{12,2},{14,0},{1,15},{3,13... | collective-permute-start | bytes 491528 | tf_op jit(solution)/shard_map/ppermute | solution.py:413
  81.4 14.2 %collective-permute-start.9 = (bf16[80,1024]{1,0:T(8,128)(2,1)}, bf16[80,1024]{1,0:T(8,128)(2,1)S(1)}, u32[]{:S(2)}, u32[]{:S(2)}) collective-permute-start(bf16[80,1024]{1,0:T(8,128)(2,1)} %get-tuple-element.39), channel_id=1, source_target_pairs={{0,2},{2,0},{4,6},{6,4},{8,10},{10,8},{12,14},{14,12},{1,3},{3,1},... | collective-permute-start | bytes 491528 | tf_op jit(solution)/shard_map/ppermute | solution.py:413
  108.8 30.4 %collective-permute-start.24 = (bf16[160,1024]{1,0:T(8,128)(2,1)S(1)}, bf16[160,1024]{1,0:T(8,128)(2,1)S(1)}, u32[]{:S(2)}, u32[]{:S(2)}) collective-permute-start(bf16[160,1024]{1,0:T(8,128)(2,1)S(1)} %collective-permute-done.23.refs_5_), channel_id=1, source_target_pairs={{0,4},{4,8},{8,12},{12,14},{14,10},{10,6},{6,2},{2,0},{16,18},{20,... | collective-permute-start | bytes 983048 | tf_op jit(solution)/shard_map/ppermute | solution.py:478
  112.2 29.3 %collective-permute-start.29 = (bf16[160,1024]{1,0:T(8,128)(2,1)S(1)}, bf16[160,1024]{1,0:T(8,128)(2,1)S(1)}, u32[]{:S(2)}, u32[]{:S(2)}) collective-permute-start(bf16[160,1024]{1,0:T(8,128)(2,1)S(1)} %collective-permute-done.28), channel_id=1, source_target_pairs={{0,4},{4,8},{8,12},{12,14},{14,10},{10,6},{6,2},{2,0},{16,18},{20,... | collective-permute-start | bytes 983048 | tf_op jit(solution)/shard_map/ppermute | solution.py:478
  167.3 14.7 %collective-permute-start.41 = (bf16[256,1024]{1,0:T(8,128)(2,1)S(1)}, bf16[256,1024]{1,0:T(8,128)(2,1)}, u32[]{:S(2)}, u32[]{:S(2)}) collective-permute-start(bf16[256,1024]{1,0:T(8,128)(2,1)S(1)} %collective-permute-done.40.refs_1_), channel_id=1, source_target_pairs={{0,4},{4,8},{8,12},{12,14},{14,10},{10,6},{6,2},{2,0},{16,18},{20,... | collective-permute-start | bytes 1572872 | tf_op jit(solution)/shard_map/ppermute | solution.py:478
  174.7 17.0 %collective-permute-start.36 = (bf16[256,1024]{1,0:T(8,128)(2,1)S(1)}, bf16[256,1024]{1,0:T(8,128)(2,1)}, u32[]{:S(2)}, u32[]{:S(2)}) collective-permute-start(bf16[256,1024]{1,0:T(8,128)(2,1)S(1)} %collective-permute-done.35.refs_0_), channel_id=1, source_target_pairs={{0,4},{4,8},{8,12},{12,14},{14,10},{10,6},{6,2},{2,0},{16,18},{20,... | collective-permute-start | bytes 1572872 | tf_op jit(solution)/shard_map/ppermute | solution.py:478
  175.5 21.8 %collective-permute-start.8 = (bf16[128,2048]{1,0:T(8,128)(2,1)}, bf16[128,2048]{1,0:T(8,128)(2,1)}, u32[]{:S(2)}, u32[]{:S(2)}) collective-permute-start(bf16[128,2048]{1,0:T(8,128)(2,1)} %get-tuple-element.36), channel_id=1, source_target_pairs={{0,2},{2,0},{4,6},{6,4},{8,10},{10,8},{12,14},{14,12},{1,3},{3,1},... | collective-permute-start | bytes 1572872 | tf_op jit(solution)/shard_map/ppermute | solution.py:420
  181.9 20.9 %collective-permute-start.42 = (bf16[256,1024]{1,0:T(8,128)(2,1)}, bf16[256,1024]{1,0:T(8,128)(2,1)}, u32[]{:S(2)}, u32[]{:S(2)}) collective-permute-start(bf16[256,1024]{1,0:T(8,128)(2,1)} %collective-permute-done.41.refs_1_), channel_id=1, source_target_pairs={{0,4},{4,8},{8,12},{12,14},{14,10},{10,6},{6,2},{2,0},{16,18},{20,... | collective-permute-start | bytes 1572872 | tf_op jit(solution)/shard_map/ppermute | solution.py:478
  191.6 16.8 %collective-permute-start.37 = (bf16[256,1024]{1,0:T(8,128)(2,1)}, bf16[256,1024]{1,0:T(8,128)(2,1)}, u32[]{:S(2)}, u32[]{:S(2)}) collective-permute-start(bf16[256,1024]{1,0:T(8,128)(2,1)} %collective-permute-done.36.refs_0_), channel_id=1, source_target_pairs={{0,4},{4,8},{8,12},{12,14},{14,10},{10,6},{6,2},{2,0},{16,18},{20,... | collective-permute-start | bytes 1572872 | tf_op jit(solution)/shard_map/ppermute | solution.py:478
  194.1 17.5 %collective-permute-start.16 = (bf16[160,2048]{1,0:T(8,128)(2,1)}, bf16[160,2048]{1,0:T(8,128)(2,1)S(1)}, u32[]{:S(2)}, u32[]{:S(2)}) collective-permute-start(bf16[160,2048]{1,0:T(8,128)(2,1)} %dynamic-slice_convert_fusion), channel_id=1, source_target_pairs={{0,1},{1,0},{2,3},{3,2},{4,5},{5,4},{6,7},{7,6},{8,9},{9,8},{10,11... | collective-permute-start | bytes 1966088 | tf_op jit(solution)/shard_map/ppermute | solution.py:496
  194.9 17.3 %collective-permute-start.48 = (bf16[256,1024]{1,0:T(8,128)(2,1)}, bf16[256,1024]{1,0:T(8,128)(2,1)}, u32[]{:S(2)}, u32[]{:S(2)}) collective-permute-start(bf16[256,1024]{1,0:T(8,128)(2,1)} %copy-done.4), channel_id=1, source_target_pairs={{0,16},{16,0},{1,17},{17,1},{2,18},{18,2},{3,19},{19,3},{4,20},{20... | collective-permute-start | bytes 1572872 | tf_op jit(solution)/shard_map/ppermute | solution.py:472
  197.3 15.1 %collective-permute-start.49 = (bf16[256,1024]{1,0:T(8,128)(2,1)}, bf16[256,1024]{1,0:T(8,128)(2,1)}, u32[]{:S(2)}, u32[]{:S(2)}) collective-permute-start(bf16[256,1024]{1,0:T(8,128)(2,1)} %collective-permute-done.41.refs_1_), channel_id=1, source_target_pairs={{0,16},{16,0},{1,17},{17,1},{2,18},{18,2},{3,19},{19,3},{4,20},{20... | collective-permute-start | bytes 1572872 | tf_op jit(solution)/shard_map/ppermute | solution.py:472
  211.7 15.3 %collective-permute-start.46 = (bf16[256,1024]{1,0:T(8,128)(2,1)}, bf16[256,1024]{1,0:T(8,128)(2,1)}, u32[]{:S(2)}, u32[]{:S(2)}) collective-permute-start(bf16[256,1024]{1,0:T(8,128)(2,1)} %collective-permute-done.36.refs_0_), channel_id=1, source_target_pairs={{0,16},{16,0},{1,17},{17,1},{2,18},{18,2},{3,19},{19,3},{4,20},{20... | collective-permute-start | bytes 1572872 | tf_op jit(solution)/shard_map/ppermute | solution.py:472
  212.3 14.7 %collective-permute-start.47 = (bf16[256,1024]{1,0:T(8,128)(2,1)}, bf16[256,1024]{1,0:T(8,128)(2,1)}, u32[]{:S(2)}, u32[]{:S(2)}) collective-permute-start(bf16[256,1024]{1,0:T(8,128)(2,1)} %collective-permute-done.42.refs_1_), channel_id=1, source_target_pairs={{0,16},{16,0},{1,17},{17,1},{2,18},{18,2},{3,19},{19,3},{4,20},{20... | collective-permute-start | bytes 1572872 | tf_op jit(solution)/shard_map/ppermute | solution.py:472
  212.3 18.3 %collective-permute-start.44 = (bf16[256,1024]{1,0:T(8,128)(2,1)}, bf16[256,1024]{1,0:T(8,128)(2,1)}, u32[]{:S(2)}, u32[]{:S(2)}) collective-permute-start(bf16[256,1024]{1,0:T(8,128)(2,1)} %collective-permute-done.37.refs_0_), channel_id=1, source_target_pairs={{0,16},{16,0},{1,17},{17,1},{2,18},{18,2},{3,19},{19,3},{4,20},{20... | collective-permute-start | bytes 1572872 | tf_op jit(solution)/shard_map/ppermute | solution.py:472
  214.1 16.5 %collective-permute-start.45 = (bf16[256,1024]{1,0:T(8,128)(2,1)}, bf16[256,1024]{1,0:T(8,128)(2,1)}, u32[]{:S(2)}, u32[]{:S(2)}) collective-permute-start(bf16[256,1024]{1,0:T(8,128)(2,1)} %collective-permute-done.43.refs_1_), channel_id=1, source_target_pairs={{0,16},{16,0},{1,17},{17,1},{2,18},{18,2},{3,19},{19,3},{4,20},{20... | collective-permute-start | bytes 1572872 | tf_op jit(solution)/shard_map/ppermute | solution.py:472
  219.7 14.6 %collective-permute-start.39 = (bf16[256,1024]{1,0:T(8,128)(2,1)}, bf16[256,1024]{1,0:T(8,128)(2,1)}, u32[]{:S(2)}, u32[]{:S(2)}) collective-permute-start(bf16[256,1024]{1,0:T(8,128)(2,1)} %collective-permute-done.38.refs_0_), channel_id=1, source_target_pairs={{0,16},{16,0},{1,17},{17,1},{2,18},{18,2},{3,19},{19,3},{4,20},{20... | collective-permute-start | bytes 1572872 | tf_op jit(solution)/shard_map/ppermute | solution.py:472
  (59 other events, 655.9 us)
